TPU v7x, 32 devices: a 4x4x1 block of a 4x4x8 slice. The times are simulated.
32 devices in a mesh: dp: 1 (over z), tp: 4 (over y), cp: 8 (over x, core).
Axes of the slice: x: 4, y: 4, z: 1, core: 2. Of those that a mesh axis runs over, the one named last changes fastest.
The devices are a block of a 4x4x8 slice.
Arguments:
- x_suffix: bfloat16 [8192, 4096], P(('dp', 'cp'))
- k_prefix: bfloat16 [8192, 8, 128], P(('dp', 'cp'), 'tp')
- v_prefix: bfloat16 [8192, 8, 128], P(('dp', 'cp'), 'tp')
- norm_attn: bfloat16 [4096], replicated
- w_query: bfloat16 [4096, 4096], P(None, 'tp')
- w_key: bfloat16 [4096, 1024], P(None, 'tp')
- w_value: bfloat16 [4096, 1024], P(None, 'tp')
- w_out: bfloat16 [4096, 4096], P('tp')
- norm_mlp: bfloat16 [4096], replicated
- w_gate: bfloat16 [4096, 14336], P(None, 'tp')
- w_up: bfloat16 [4096, 14336], P(None, 'tp')
- w_down: bfloat16 [14336, 4096], P('tp')
Outputs:
- output 1: bfloat16 [8192, 4096], P(('dp', 'cp'))
- output 2: bfloat16 [8192, 8, 128], P(('dp', 'cp'), 'tp')
- output 3: bfloat16 [8192, 8, 128], P(('dp', 'cp'), 'tp')
All inputs are finite; a program needn't handle non-finite values.
Results may differ from a plain program's by a relative error of at most 0.0110871.
Values are sent between devices in bfloat16 or wider.
A program may use at most 768 MiB of HBM per device.

v0:
```python
import jax
import jax.numpy as jnp
from jax import lax
from jax.sharding import PartitionSpec as P

ROPE_THETA = 500000.0
NORM_EPS = 1e-5


def block_positions(owner, groups, blk_len, prefix_len):
    local_row = jnp.arange(2 * blk_len, dtype=jnp.int32)
    blk_idx = jnp.where(local_row < blk_len, owner, 2 * groups - 1 - owner)
    return prefix_len + blk_idx * blk_len + local_row % blk_len


def rope_tables(positions, head_dim):
    inv_freq = ROPE_THETA ** (-jnp.arange(0, head_dim, 2, dtype=jnp.float32) / head_dim)
    angles = positions.astype(jnp.float32)[:, None] * inv_freq[None, :]
    return jnp.cos(angles), jnp.sin(angles)


def apply_rope(values, cos_tab, sin_tab):
    half_dim = values.shape[-1] // 2
    first_half = values[..., :half_dim]
    second_half = values[..., half_dim:]
    cos_rows = cos_tab[:, None, :]
    sin_rows = sin_tab[:, None, :]
    return jnp.concatenate([first_half * cos_rows - second_half * sin_rows, second_half * cos_rows + first_half * sin_rows], axis=-1)


def rms_norm(values, gain_vec):
    vals32 = values.astype(jnp.float32)
    inv_rms = lax.rsqrt(jnp.mean(vals32 * vals32, axis=-1, keepdims=True) + NORM_EPS)
    return (vals32 * inv_rms * gain_vec.astype(jnp.float32)).astype(jnp.bfloat16)


def attend_step(acc_state, q_rot, k_blk, v_blk, q_pos, k_pos, score_scale):
    row_max, denom_sum, numer_sum = acc_state
    scores = jnp.einsum('sgrd,kgd->sgrk', q_rot, k_blk, preferred_element_type=jnp.float32) * score_scale
    visible = (k_pos[None, :] <= q_pos[:, None])[:, None, None, :]
    scores = jnp.where(visible, scores, -jnp.inf)
    new_max = jnp.maximum(row_max, jnp.max(scores, axis=-1))
    correction = jnp.exp(row_max - new_max)
    weights = jnp.exp(scores - new_max[..., None])
    denom_sum = denom_sum * correction + jnp.sum(weights, axis=-1)
    numer_sum = numer_sum * correction[..., None] + jnp.einsum('sgrk,kgd->sgrd', weights.astype(jnp.bfloat16), v_blk, preferred_element_type=jnp.float32)
    return new_max, denom_sum, numer_sum


def solution(mesh):
    groups = mesh.shape['cp']

    def local_layer(x_loc, kp_loc, vp_loc, norm_attn, w_query, w_key, w_value, w_out, norm_mlp, w_gate, w_up, w_down):
        rows_loc = x_loc.shape[0]
        blk_len = rows_loc // 2
        pre_dev, kv_loc, head_dim = kp_loc.shape
        heads_loc = w_query.shape[1] // head_dim
        group_ratio = heads_loc // kv_loc
        prefix_len = pre_dev * groups
        my_idx = lax.axis_index('cp')
        q_pos = block_positions(my_idx, groups, blk_len, prefix_len)
        cos_tab, sin_tab = rope_tables(q_pos, head_dim)
        hidden = rms_norm(x_loc, norm_attn)
        q_proj = jnp.dot(hidden, w_query, preferred_element_type=jnp.float32).reshape(rows_loc, heads_loc, head_dim)
        q_rot = apply_rope(q_proj, cos_tab, sin_tab).astype(jnp.bfloat16).reshape(rows_loc, kv_loc, group_ratio, head_dim)
        k_proj = jnp.dot(hidden, w_key, preferred_element_type=jnp.float32).reshape(rows_loc, kv_loc, head_dim)
        k_new = apply_rope(k_proj, cos_tab, sin_tab).astype(jnp.bfloat16)
        v_new = jnp.dot(hidden, w_value, preferred_element_type=jnp.float32).astype(jnp.bfloat16).reshape(rows_loc, kv_loc, head_dim)
        k_bundle = jnp.concatenate([kp_loc, k_new], axis=0)
        v_bundle = jnp.concatenate([vp_loc, v_new], axis=0)
        pre_offsets = jnp.arange(pre_dev, dtype=jnp.int32)

        def key_positions(src_idx):
            return jnp.concatenate([src_idx * pre_dev + pre_offsets, block_positions(src_idx, groups, blk_len, prefix_len)])

        score_scale = head_dim ** -0.5
        stat_shape = (rows_loc, kv_loc, group_ratio)
        init_state = (jnp.full(stat_shape, -jnp.inf, dtype=jnp.float32), jnp.zeros(stat_shape, jnp.float32), jnp.zeros(stat_shape + (head_dim,), jnp.float32))
        first_state = attend_step(init_state, q_rot, k_bundle, v_bundle, q_pos, key_positions(my_idx), score_scale)
        perm_pairs = [(dev_idx, (dev_idx + 1) % groups) for dev_idx in range(groups)]

        def step_body(step_idx, loop_state):
            k_cur, v_cur, acc_state = loop_state
            k_cur, v_cur = lax.ppermute((k_cur, v_cur), 'cp', perm_pairs)
            src_idx = (my_idx - step_idx) % groups
            acc_state = attend_step(acc_state, q_rot, k_cur, v_cur, q_pos, key_positions(src_idx), score_scale)
            return k_cur, v_cur, acc_state

        final_state = lax.fori_loop(1, groups, step_body, (k_bundle, v_bundle, first_state))[2]
        attn_heads = (final_state[2] / final_state[1][..., None]).astype(jnp.bfloat16).reshape(rows_loc, heads_loc * head_dim)
        resid_mid = x_loc.astype(jnp.float32) + lax.psum(jnp.dot(attn_heads, w_out, preferred_element_type=jnp.float32), 'tp')
        hidden_mlp = rms_norm(resid_mid, norm_mlp)
        gate_proj = jnp.dot(hidden_mlp, w_gate, preferred_element_type=jnp.float32)
        up_proj = jnp.dot(hidden_mlp, w_up, preferred_element_type=jnp.float32)
        act_mid = (jax.nn.silu(gate_proj) * up_proj).astype(jnp.bfloat16)
        x_out = (resid_mid + lax.psum(jnp.dot(act_mid, w_down, preferred_element_type=jnp.float32), 'tp')).astype(jnp.bfloat16)
        return x_out, k_new, v_new

    row_spec = P(('dp', 'cp'), None)
    kv_spec = P(('dp', 'cp'), 'tp', None)
    col_spec = P(None, 'tp')
    row_split = P('tp', None)
    vec_spec = P(None)
    return jax.shard_map(local_layer, mesh=mesh, in_specs=(row_spec, kv_spec, kv_spec, vec_spec, col_spec, col_spec, col_spec, row_split, vec_spec, col_spec, col_spec, row_split), out_specs=(row_spec, kv_spec, kv_spec), check_vma=False)
```

profile of v0, /device:TPU:96, one launch (start us, length us, event | category | flops | bytes accessed | tf_op | source)
XLA Modules:
  0.0 1563.2 jit_solution(4112089196790044047)
XLA Ops:
  50.2 26.7 %fusion.23 = (f32[1024,2,4]{0,2,1:T(4,128)S(1)}, f32[2,2048,1024,4]{2,1,3,0:T(8,128)}) fusion(pred[1024,2048]{0,1:T(8,128)(4,1)S(1)} %broadcast_compare_fusion.1, bf16[1024,2,4,128]{3,0,2,1:T(8,128)(2,1)} %pad_maximum_fusion, bf16[2048,2,128]{2,0,1:T(8,128)(2,1)} %maximum_maximum_fusion), kind=kOutput, calls=%fused_computation.32 | convolution fusion | flops 4345290752 | bytes 72384512 | tf_op jit(solution)/shard_map/sgrd,kgd->sgrk/dot_general | solution.py:39
  77.0 21.6 %fusion.22 = f32[1024,2,4]{0,2,1:T(4,128)S(1)} fusion(f32[2,2048,1024,4]{2,1,3,0:T(8,128)} %get-tuple-element.399, f32[1024,2,4]{0,2,1:T(4,128)S(1)} %get-tuple-element.476, pred[1024,2048]{0,1:T(8,128)(4,1)S(1)} %broadcast_compare_fusion.1), kind=kLoop, calls=%fused_computation.31 | loop fusion | flops 67100672 | bytes 69271552 | tf_op jit(solution)/shard_map/reduce_sum | solution.py:45
  108.5 27.0 %bitcast_add_fusion.1 = f32[1024,2,4,128]{0,3,2,1:T(8,128)} fusion(f32[2,2048,1024,4]{2,1,3,0:T(8,128)} %get-tuple-element.399, f32[1024,2,4]{0,2,1:T(4,128)S(1)} %get-tuple-element.476, pred[1024,2048]{0,1:T(8,128)(4,1)S(1)} %broadcast_compare_fusion.1, f32[1024,2,4]{0,2,1:T(4,128)S(1)} %get-tuple-element.394, bf16[1024,2,128]{0,2,1:T(8,128)(2,1)} %bitcast.116, ...), kind=kOutput, calls=%fused_computation.47 | convolution fusion | flops 4365221888 | bytes 74514432 | tf_op jit(solution)/shard_map/sgrk,kgd->sgrd/dot_general | solution.py:46
  142.1 666.1 %while.26 = (s32[]{:T(128)}, bf16[2048,2,128]{2,0,1:T(8,128)(2,1)}, bf16[2048,2,128]{2,0,1:T(8,128)(2,1)}, f32[1024,2,4]{0,2,1:T(4,128)S(1)}, f32[1024,2,4]{0,2,...) while((s32[]{:T(128)}, bf16[2048,2,128]{2,0,1:T(8,128)(2,1)}, ...), condition=%wide.region_6.7_spmd.clone.clone, body=%wide.region_3.6_spmd.clone.clone.sunk | while | flops 8778720256 | bytes 235446672 | solution.py:89
  157.8 26.3 %fusion.82 = (f32[1024,2,4]{0,2,1:T(4,128)S(1)}, f32[2,2048,1024,4]{2,1,3,0:T(8,128)}) fusion(pred[1024,2048]{0,1:T(8,128)(4,1)S(1)} %broadcast_compare_fusion.3, bf16[1024,2,4,128]{3,0,2,1:T(8,128)(2,1)} %get-tuple-element.510, bf16[2048,2,128]{2,0,1:T(8,128)(2,1)} %collective-permute-done), kind=kOutput, calls=%fused_computation.6.clone.1 | convolution fusion | flops 4345290752 | bytes 72384512 | tf_op jit(solution)/shard_map/while/body/eval_jaxpr/sgrd,kgd->sgrk/dot_general | solution.py:39
  184.1 21.6 %fusion.83 = f32[1024,2,4]{0,2,1:T(4,128)S(1)} fusion(f32[2,2048,1024,4]{2,1,3,0:T(8,128)} %get-tuple-element.470, f32[1024,2,4]{0,2,1:T(4,128)S(1)} %max.14, pred[1024,2048]{0,1:T(8,128)(4,1)S(1)} %broadcast_compare_fusion.3), kind=kLoop, calls=%fused_computation.5.clone.1 | loop fusion | flops 67100672 | bytes 69271552 | tf_op jit(solution)/shard_map/while/body/eval_jaxpr/reduce_sum | solution.py:45
  208.9 28.5 %bitcast_add_fusion.3 = f32[1024,2,4,128]{3,0,2,1:T(8,128)} fusion(f32[1024,2,4,128]{3,0,2,1:T(8,128)} %get-tuple-element.493, f32[2,2048,1024,4]{2,1,3,0:T(8,128)} %get-tuple-element.470, f32[1024,2,4]{0,2,1:T(4,128)S(1)} %max.14, pred[1024,2048]{0,1:T(8,128)(4,1)S(1)} %broadcast_compare_fusion.3, f32[1024,2,4]{0,2,1:T(4,128)S(1)} %bitcast.121, ...), kind=kOutput, calls=%fused_computation.9.clone.1 | convolution fusion | flops 4364173312 | bytes 78708736 | tf_op jit(solution)/shard_map/while/body/eval_jaxpr/sgrk,kgd->sgrd/dot_general | solution.py:46
  252.9 26.3 %fusion.82 = (f32[1024,2,4]{0,2,1:T(4,128)S(1)}, f32[2,2048,1024,4]{2,1,3,0:T(8,128)}) fusion(pred[1024,2048]{0,1:T(8,128)(4,1)S(1)} %broadcast_compare_fusion.3, bf16[1024,2,4,128]{3,0,2,1:T(8,128)(2,1)} %get-tuple-element.510, bf16[2048,2,128]{2,0,1:T(8,128)(2,1)} %collective-permute-done), kind=kOutput, calls=%fused_computation.6.clone.1 | convolution fusion | flops 4345290752 | bytes 72384512 | tf_op jit(solution)/shard_map/while/body/eval_jaxpr/sgrd,kgd->sgrk/dot_general | solution.py:39
  279.2 21.6 %fusion.83 = f32[1024,2,4]{0,2,1:T(4,128)S(1)} fusion(f32[2,2048,1024,4]{2,1,3,0:T(8,128)} %get-tuple-element.470, f32[1024,2,4]{0,2,1:T(4,128)S(1)} %max.14, pred[1024,2048]{0,1:T(8,128)(4,1)S(1)} %broadcast_compare_fusion.3), kind=kLoop, calls=%fused_computation.5.clone.1 | loop fusion | flops 67100672 | bytes 69271552 | tf_op jit(solution)/shard_map/while/body/eval_jaxpr/reduce_sum | solution.py:45
  304.1 28.5 %bitcast_add_fusion.3 = f32[1024,2,4,128]{3,0,2,1:T(8,128)} fusion(f32[1024,2,4,128]{3,0,2,1:T(8,128)} %get-tuple-element.493, f32[2,2048,1024,4]{2,1,3,0:T(8,128)} %get-tuple-element.470, f32[1024,2,4]{0,2,1:T(4,128)S(1)} %max.14, pred[1024,2048]{0,1:T(8,128)(4,1)S(1)} %broadcast_compare_fusion.3, f32[1024,2,4]{0,2,1:T(4,128)S(1)} %bitcast.121, ...), kind=kOutput, calls=%fused_computation.9.clone.1 | convolution fusion | flops 4364173312 | bytes 78708736 | tf_op jit(solution)/shard_map/while/body/eval_jaxpr/sgrk,kgd->sgrd/dot_general | solution.py:46
  348.0 26.3 %fusion.82 = (f32[1024,2,4]{0,2,1:T(4,128)S(1)}, f32[2,2048,1024,4]{2,1,3,0:T(8,128)}) fusion(pred[1024,2048]{0,1:T(8,128)(4,1)S(1)} %broadcast_compare_fusion.3, bf16[1024,2,4,128]{3,0,2,1:T(8,128)(2,1)} %get-tuple-element.510, bf16[2048,2,128]{2,0,1:T(8,128)(2,1)} %collective-permute-done), kind=kOutput, calls=%fused_computation.6.clone.1 | convolution fusion | flops 4345290752 | bytes 72384512 | tf_op jit(solution)/shard_map/while/body/eval_jaxpr/sgrd,kgd->sgrk/dot_general | solution.py:39
  374.3 21.6 %fusion.83 = f32[1024,2,4]{0,2,1:T(4,128)S(1)} fusion(f32[2,2048,1024,4]{2,1,3,0:T(8,128)} %get-tuple-element.470, f32[1024,2,4]{0,2,1:T(4,128)S(1)} %max.14, pred[1024,2048]{0,1:T(8,128)(4,1)S(1)} %broadcast_compare_fusion.3), kind=kLoop, calls=%fused_computation.5.clone.1 | loop fusion | flops 67100672 | bytes 69271552 | tf_op jit(solution)/shard_map/while/body/eval_jaxpr/reduce_sum | solution.py:45
  399.2 28.5 %bitcast_add_fusion.3 = f32[1024,2,4,128]{3,0,2,1:T(8,128)} fusion(f32[1024,2,4,128]{3,0,2,1:T(8,128)} %get-tuple-element.493, f32[2,2048,1024,4]{2,1,3,0:T(8,128)} %get-tuple-element.470, f32[1024,2,4]{0,2,1:T(4,128)S(1)} %max.14, pred[1024,2048]{0,1:T(8,128)(4,1)S(1)} %broadcast_compare_fusion.3, f32[1024,2,4]{0,2,1:T(4,128)S(1)} %bitcast.121, ...), kind=kOutput, calls=%fused_computation.9.clone.1 | convolution fusion | flops 4364173312 | bytes 78708736 | tf_op jit(solution)/shard_map/while/body/eval_jaxpr/sgrk,kgd->sgrd/dot_general | solution.py:46
  443.1 26.3 %fusion.82 = (f32[1024,2,4]{0,2,1:T(4,128)S(1)}, f32[2,2048,1024,4]{2,1,3,0:T(8,128)}) fusion(pred[1024,2048]{0,1:T(8,128)(4,1)S(1)} %broadcast_compare_fusion.3, bf16[1024,2,4,128]{3,0,2,1:T(8,128)(2,1)} %get-tuple-element.510, bf16[2048,2,128]{2,0,1:T(8,128)(2,1)} %collective-permute-done), kind=kOutput, calls=%fused_computation.6.clone.1 | convolution fusion | flops 4345290752 | bytes 72384512 | tf_op jit(solution)/shard_map/while/body/eval_jaxpr/sgrd,kgd->sgrk/dot_general | solution.py:39
  469.4 21.6 %fusion.83 = f32[1024,2,4]{0,2,1:T(4,128)S(1)} fusion(f32[2,2048,1024,4]{2,1,3,0:T(8,128)} %get-tuple-element.470, f32[1024,2,4]{0,2,1:T(4,128)S(1)} %max.14, pred[1024,2048]{0,1:T(8,128)(4,1)S(1)} %broadcast_compare_fusion.3), kind=kLoop, calls=%fused_computation.5.clone.1 | loop fusion | flops 67100672 | bytes 69271552 | tf_op jit(solution)/shard_map/while/body/eval_jaxpr/reduce_sum | solution.py:45
  494.3 28.5 %bitcast_add_fusion.3 = f32[1024,2,4,128]{3,0,2,1:T(8,128)} fusion(f32[1024,2,4,128]{3,0,2,1:T(8,128)} %get-tuple-element.493, f32[2,2048,1024,4]{2,1,3,0:T(8,128)} %get-tuple-element.470, f32[1024,2,4]{0,2,1:T(4,128)S(1)} %max.14, pred[1024,2048]{0,1:T(8,128)(4,1)S(1)} %broadcast_compare_fusion.3, f32[1024,2,4]{0,2,1:T(4,128)S(1)} %bitcast.121, ...), kind=kOutput, calls=%fused_computation.9.clone.1 | convolution fusion | flops 4364173312 | bytes 78708736 | tf_op jit(solution)/shard_map/while/body/eval_jaxpr/sgrk,kgd->sgrd/dot_general | solution.py:46
  538.3 26.3 %fusion.82 = (f32[1024,2,4]{0,2,1:T(4,128)S(1)}, f32[2,2048,1024,4]{2,1,3,0:T(8,128)}) fusion(pred[1024,2048]{0,1:T(8,128)(4,1)S(1)} %broadcast_compare_fusion.3, bf16[1024,2,4,128]{3,0,2,1:T(8,128)(2,1)} %get-tuple-element.510, bf16[2048,2,128]{2,0,1:T(8,128)(2,1)} %collective-permute-done), kind=kOutput, calls=%fused_computation.6.clone.1 | convolution fusion | flops 4345290752 | bytes 72384512 | tf_op jit(solution)/shard_map/while/body/eval_jaxpr/sgrd,kgd->sgrk/dot_general | solution.py:39
  564.6 21.6 %fusion.83 = f32[1024,2,4]{0,2,1:T(4,128)S(1)} fusion(f32[2,2048,1024,4]{2,1,3,0:T(8,128)} %get-tuple-element.470, f32[1024,2,4]{0,2,1:T(4,128)S(1)} %max.14, pred[1024,2048]{0,1:T(8,128)(4,1)S(1)} %broadcast_compare_fusion.3), kind=kLoop, calls=%fused_computation.5.clone.1 | loop fusion | flops 67100672 | bytes 69271552 | tf_op jit(solution)/shard_map/while/body/eval_jaxpr/reduce_sum | solution.py:45
  589.4 28.5 %bitcast_add_fusion.3 = f32[1024,2,4,128]{3,0,2,1:T(8,128)} fusion(f32[1024,2,4,128]{3,0,2,1:T(8,128)} %get-tuple-element.493, f32[2,2048,1024,4]{2,1,3,0:T(8,128)} %get-tuple-element.470, f32[1024,2,4]{0,2,1:T(4,128)S(1)} %max.14, pred[1024,2048]{0,1:T(8,128)(4,1)S(1)} %broadcast_compare_fusion.3, f32[1024,2,4]{0,2,1:T(4,128)S(1)} %bitcast.121, ...), kind=kOutput, calls=%fused_computation.9.clone.1 | convolution fusion | flops 4364173312 | bytes 78708736 | tf_op jit(solution)/shard_map/while/body/eval_jaxpr/sgrk,kgd->sgrd/dot_general | solution.py:46
  633.4 26.3 %fusion.82 = (f32[1024,2,4]{0,2,1:T(4,128)S(1)}, f32[2,2048,1024,4]{2,1,3,0:T(8,128)}) fusion(pred[1024,2048]{0,1:T(8,128)(4,1)S(1)} %broadcast_compare_fusion.3, bf16[1024,2,4,128]{3,0,2,1:T(8,128)(2,1)} %get-tuple-element.510, bf16[2048,2,128]{2,0,1:T(8,128)(2,1)} %collective-permute-done), kind=kOutput, calls=%fused_computation.6.clone.1 | convolution fusion | flops 4345290752 | bytes 72384512 | tf_op jit(solution)/shard_map/while/body/eval_jaxpr/sgrd,kgd->sgrk/dot_general | solution.py:39
  659.7 21.6 %fusion.83 = f32[1024,2,4]{0,2,1:T(4,128)S(1)} fusion(f32[2,2048,1024,4]{2,1,3,0:T(8,128)} %get-tuple-element.470, f32[1024,2,4]{0,2,1:T(4,128)S(1)} %max.14, pred[1024,2048]{0,1:T(8,128)(4,1)S(1)} %broadcast_compare_fusion.3), kind=kLoop, calls=%fused_computation.5.clone.1 | loop fusion | flops 67100672 | bytes 69271552 | tf_op jit(solution)/shard_map/while/body/eval_jaxpr/reduce_sum | solution.py:45
  684.6 28.5 %bitcast_add_fusion.3 = f32[1024,2,4,128]{3,0,2,1:T(8,128)} fusion(f32[1024,2,4,128]{3,0,2,1:T(8,128)} %get-tuple-element.493, f32[2,2048,1024,4]{2,1,3,0:T(8,128)} %get-tuple-element.470, f32[1024,2,4]{0,2,1:T(4,128)S(1)} %max.14, pred[1024,2048]{0,1:T(8,128)(4,1)S(1)} %broadcast_compare_fusion.3, f32[1024,2,4]{0,2,1:T(4,128)S(1)} %bitcast.121, ...), kind=kOutput, calls=%fused_computation.9.clone.1 | convolution fusion | flops 4364173312 | bytes 78708736 | tf_op jit(solution)/shard_map/while/body/eval_jaxpr/sgrk,kgd->sgrd/dot_general | solution.py:46
  728.5 26.3 %fusion.82 = (f32[1024,2,4]{0,2,1:T(4,128)S(1)}, f32[2,2048,1024,4]{2,1,3,0:T(8,128)}) fusion(pred[1024,2048]{0,1:T(8,128)(4,1)S(1)} %broadcast_compare_fusion.3, bf16[1024,2,4,128]{3,0,2,1:T(8,128)(2,1)} %get-tuple-element.510, bf16[2048,2,128]{2,0,1:T(8,128)(2,1)} %collective-permute-done), kind=kOutput, calls=%fused_computation.6.clone.1 | convolution fusion | flops 4345290752 | bytes 72384512 | tf_op jit(solution)/shard_map/while/body/eval_jaxpr/sgrd,kgd->sgrk/dot_general | solution.py:39
  754.8 21.6 %fusion.83 = f32[1024,2,4]{0,2,1:T(4,128)S(1)} fusion(f32[2,2048,1024,4]{2,1,3,0:T(8,128)} %get-tuple-element.470, f32[1024,2,4]{0,2,1:T(4,128)S(1)} %max.14, pred[1024,2048]{0,1:T(8,128)(4,1)S(1)} %broadcast_compare_fusion.3), kind=kLoop, calls=%fused_computation.5.clone.1 | loop fusion | flops 67100672 | bytes 69271552 | tf_op jit(solution)/shard_map/while/body/eval_jaxpr/reduce_sum | solution.py:45
  779.7 28.5 %bitcast_add_fusion.3 = f32[1024,2,4,128]{3,0,2,1:T(8,128)} fusion(f32[1024,2,4,128]{3,0,2,1:T(8,128)} %get-tuple-element.493, f32[2,2048,1024,4]{2,1,3,0:T(8,128)} %get-tuple-element.470, f32[1024,2,4]{0,2,1:T(4,128)S(1)} %max.14, pred[1024,2048]{0,1:T(8,128)(4,1)S(1)} %broadcast_compare_fusion.3, f32[1024,2,4]{0,2,1:T(4,128)S(1)} %bitcast.121, ...), kind=kOutput, calls=%fused_computation.9.clone.1 | convolution fusion | flops 4364173312 | bytes 78708736 | tf_op jit(solution)/shard_map/while/body/eval_jaxpr/sgrk,kgd->sgrd/dot_general | solution.py:46
  816.3 14.6 fusion.52
  831.6 289.5 %all-reduce.3.cloned.1.call-done = f32[1024,4096]{1,0:T(8,128)} async-done(((f32[1024,4096]{1,0:T(8,128)}), f32[1024,4096]{1,0:T(8,128)}) %all-reduce.3.cloned.1.call-update) | async-done | bytes 16777232 | tf_op jit(solution)/shard_map/psum | solution.py:91
  1140.3 35.2 %fusion.53 = f32[1024,3584]{1,0:T(8,128)} fusion(bf16[1024,4096]{1,0:T(8,128)(2,1)S(1)} %multiply_convert_fusion, bf16[4096,3584]{1,0:T(8,128)(2,1)} %param.23), kind=kOutput, calls=%fused_computation.86 | convolution fusion | flops 30064771072 | bytes 52428800 | tf_op jit(solution)/shard_map/dot_general | solution.py:93
  1175.5 36.2 %multiply_convert_fusion.1.clone.4 = bf16[1024,3584]{1,0:T(8,128)(2,1)S(1)} fusion(f32[1024,3584]{1,0:T(8,128)} %fusion.53, bf16[1024,4096]{1,0:T(8,128)(2,1)S(1)} %multiply_convert_fusion, bf16[4096,3584]{1,0:T(8,128)(2,1)} %param.24), kind=kOutput, calls=%fused_computation.44.clone.clone.clone.1 | convolution fusion | flops 30086791168 | bytes 59768832 | tf_op jit(solution)/shard_map/dot_general | solution.py:94
  1211.7 36.2 %fusion.30 = f32[1024,4096]{1,0:T(8,128)} fusion(bf16[3584,4096]{1,0:T(8,128)(2,1)} %param.25, bf16[1024,3584]{1,0:T(8,128)(2,1)S(1)} %multiply_convert_fusion.1.clone.4), kind=kOutput, calls=%fused_computation.45 | convolution fusion | flops 30064771072 | bytes 53477376 | tf_op jit(solution)/shard_map/dot_general | solution.py:96
  1251.7 286.5 %all-reduce.5.cloned.1.call-done = f32[1024,4096]{1,0:T(8,128)} async-done(((f32[1024,4096]{1,0:T(8,128)}), f32[1024,4096]{1,0:T(8,128)}) %all-reduce.5.cloned.1.call-update) | async-done | bytes 16777232 | tf_op jit(solution)/shard_map/psum | solution.py:96
  1538.3 17.8 %add_convert_fusion = bf16[1024,4096]{1,0:T(8,128)(2,1)} fusion(f32[1024,4096]{1,0:T(8,128)} %all-reduce.5.cloned.1.call-done, f32[1024,4096]{1,0:T(8,128)} %all-reduce.3.cloned.1.call-done, bf16[1024,4096]{1,0:T(8,128)(2,1)} %param.14), kind=kLoop, calls=%fused_computation.41 | loop fusion | flops 16777216 | bytes 50331648 | tf_op jit(solution)/shard_map/convert_element_type | solution.py:96
  (167 shorter events, 221.9 us)
Async XLA Ops:
  7.2 9.2 copy-start
  7.2 1114.0 %all-reduce.3.cloned.1.call-start = ((), (), s32[]{:S(2)}) async-start(), calls=%async_computation | async-start | bytes 33554432 | tf_op jit(solution)/shard_map/psum | solution.py:91
  8.3 11.0 copy-start.9
  10.3 6.1 copy-start.3
  23.0 14.2 copy-start.10
  41.5 6.1 copy-start.8
  41.5 6.1 copy-start.13
  41.5 6.1 copy-start.14
  41.5 7.4 copy-start.11
  47.9 0.8 copy-start.4
  47.9 1.0 copy-start.6
  98.6 7.5 copy-start.15
  142.3 15.5 collective-permute-start
  142.4 65.6 %collective-permute-start.1 = (bf16[2048,2,128]{2,0,1:T(8,128)(2,1)}, bf16[2048,2,128]{2,0,1:T(8,128)(2,1)S(1)}, u32[]{:S(2)}, u32[]{:S(2)}) collective-permute-start(bf16[2048,2,128]{2,0,1:T(8,128)(2,1)} %get-tuple-element.490), channel_id=1, source_target_pairs={{0,1},{1,2},{2,3},{3,4},{4,5},{5,6},{6,7},{7,0},{8,9},{9,10},{10,1... | collective-permute-start | bytes 3145736 | tf_op jit(solution)/shard_map/while/body/eval_jaxpr/ppermute | solution.py:84
  237.5 15.4 collective-permute-start
  237.5 65.6 %collective-permute-start.1 = (bf16[2048,2,128]{2,0,1:T(8,128)(2,1)}, bf16[2048,2,128]{2,0,1:T(8,128)(2,1)S(1)}, u32[]{:S(2)}, u32[]{:S(2)}) collective-permute-start(bf16[2048,2,128]{2,0,1:T(8,128)(2,1)} %get-tuple-element.490), channel_id=1, source_target_pairs={{0,1},{1,2},{2,3},{3,4},{4,5},{5,6},{6,7},{7,0},{8,9},{9,10},{10,1... | collective-permute-start | bytes 3145736 | tf_op jit(solution)/shard_map/while/body/eval_jaxpr/ppermute | solution.py:84
  332.6 15.4 collective-permute-start
  332.6 65.6 %collective-permute-start.1 = (bf16[2048,2,128]{2,0,1:T(8,128)(2,1)}, bf16[2048,2,128]{2,0,1:T(8,128)(2,1)S(1)}, u32[]{:S(2)}, u32[]{:S(2)}) collective-permute-start(bf16[2048,2,128]{2,0,1:T(8,128)(2,1)} %get-tuple-element.490), channel_id=1, source_target_pairs={{0,1},{1,2},{2,3},{3,4},{4,5},{5,6},{6,7},{7,0},{8,9},{9,10},{10,1... | collective-permute-start | bytes 3145736 | tf_op jit(solution)/shard_map/while/body/eval_jaxpr/ppermute | solution.py:84
  427.7 15.4 collective-permute-start
  427.7 65.6 %collective-permute-start.1 = (bf16[2048,2,128]{2,0,1:T(8,128)(2,1)}, bf16[2048,2,128]{2,0,1:T(8,128)(2,1)S(1)}, u32[]{:S(2)}, u32[]{:S(2)}) collective-permute-start(bf16[2048,2,128]{2,0,1:T(8,128)(2,1)} %get-tuple-element.490), channel_id=1, source_target_pairs={{0,1},{1,2},{2,3},{3,4},{4,5},{5,6},{6,7},{7,0},{8,9},{9,10},{10,1... | collective-permute-start | bytes 3145736 | tf_op jit(solution)/shard_map/while/body/eval_jaxpr/ppermute | solution.py:84
  522.8 15.4 collective-permute-start
  522.8 65.6 %collective-permute-start.1 = (bf16[2048,2,128]{2,0,1:T(8,128)(2,1)}, bf16[2048,2,128]{2,0,1:T(8,128)(2,1)S(1)}, u32[]{:S(2)}, u32[]{:S(2)}) collective-permute-start(bf16[2048,2,128]{2,0,1:T(8,128)(2,1)} %get-tuple-element.490), channel_id=1, source_target_pairs={{0,1},{1,2},{2,3},{3,4},{4,5},{5,6},{6,7},{7,0},{8,9},{9,10},{10,1... | collective-permute-start | bytes 3145736 | tf_op jit(solution)/shard_map/while/body/eval_jaxpr/ppermute | solution.py:84
  618.0 15.4 collective-permute-start
  618.0 65.6 %collective-permute-start.1 = (bf16[2048,2,128]{2,0,1:T(8,128)(2,1)}, bf16[2048,2,128]{2,0,1:T(8,128)(2,1)S(1)}, u32[]{:S(2)}, u32[]{:S(2)}) collective-permute-start(bf16[2048,2,128]{2,0,1:T(8,128)(2,1)} %get-tuple-element.490), channel_id=1, source_target_pairs={{0,1},{1,2},{2,3},{3,4},{4,5},{5,6},{6,7},{7,0},{8,9},{9,10},{10,1... | collective-permute-start | bytes 3145736 | tf_op jit(solution)/shard_map/while/body/eval_jaxpr/ppermute | solution.py:84
  713.1 15.4 collective-permute-start
  713.1 65.6 %collective-permute-start.1 = (bf16[2048,2,128]{2,0,1:T(8,128)(2,1)}, bf16[2048,2,128]{2,0,1:T(8,128)(2,1)S(1)}, u32[]{:S(2)}, u32[]{:S(2)}) collective-permute-start(bf16[2048,2,128]{2,0,1:T(8,128)(2,1)} %get-tuple-element.490), channel_id=1, source_target_pairs={{0,1},{1,2},{2,3},{3,4},{4,5},{5,6},{6,7},{7,0},{8,9},{9,10},{10,1... | collective-permute-start | bytes 3145736 | tf_op jit(solution)/shard_map/while/body/eval_jaxpr/ppermute | solution.py:84
  831.0 707.2 %all-reduce.5.cloned.1.call-start = ((), (), s32[]{:S(2)}) async-start(), calls=%async_computation.1 | async-start | bytes 33554432 | tf_op jit(solution)/shard_map/psum | solution.py:96
  1121.2 13.0 copy-start.2
  1248.0 1.0 copy-start.12
  1248.0 2.1 copy-start.5
  1248.0 2.1 copy-start.7
  1538.3 17.8 %copy-start.1 = (bf16[4096,256]{1,0:T(8,128)(2,1)S(1)}, bf16[4096,256]{1,0:T(8,128)(2,1)}, u32[]{:S(2)}) copy-start(bf16[4096,256]{1,0:T(8,128)(2,1)} %param.19) | copy-start | bytes 6291460
  (1 other events, 0.7 us)
Sparse Core Ops, SparseCore 0:
  831.1 289.9 all-reduce.2
  1248.1 290.0 all-reduce.4
where the time goes:
time: 1570 us; the launch traced here: 1560 us
  waiting for transfers between devices  673 us (43%)
  matrix products  584 us (37%)
  other arithmetic  236 us (15%)
  local copies, waits for them, and re-layouts  53.6 us (3%)
    psum x1, waiting for transfers between devices, local_layer(): lax.psum(jnp.dot(attn_heads, w_out, preferred_element_type=jnp.float32),...  290 us
    psum x1, waiting for transfers between devices, local_layer(): lax.psum(jnp.dot(act_mid, w_down, preferred_element_type=jnp.float32), 'tp')  287 us
    dot_general x8, matrix products, attend_step(): jnp.einsum('sgrk,kgd->sgrd', weights.astype(jnp.bfloat16), v_blk, preferr...  227 us
    dot_general x8, matrix products, attend_step(): jnp.einsum('sgrd,kgd->sgrk', q_rot, k_blk, preferred_element_type=jnp.flo...  211 us
    reduce_sum x8, other arithmetic, attend_step(): denom_sum = denom_sum * correction + jnp.sum(weights, axis=-1)  173 us
    ppermute x14, waiting for transfers between devices, step_body(): k_cur, v_cur = lax.ppermute((k_cur, v_cur), 'cp', perm_pairs)  97 us
    dot_general x1, matrix products, local_layer(): jnp.dot(act_mid, w_down, preferred_element_type=jnp.float32)  36.2 us
    dot_general x1, matrix products, local_layer(): up_proj = jnp.dot(hidden_mlp, w_up, preferred_element_type=jnp.float32)  36.2 us
  transfers between devices with their start and end apart: 16, of which 9 were waited for; matrix products, arithmetic and copies ran while one was open for 23% of the time, Pallas kernels for 0%

commit v1 on v0

v1 whole, which is shorter than its diff:
```python
import functools

import jax
import jax.numpy as jnp
from jax import lax
from jax.experimental import pallas as pl
from jax.experimental.pallas import tpu as pltpu
from jax.sharding import PartitionSpec as P

ROPE_THETA = 500000.0
NORM_EPS = 1e-5
LOG2E = 1.4426950408889634
KEY_BLOCK = 512


def rope_tables(positions, head_dim):
    inv_freq = ROPE_THETA ** (-jnp.arange(0, head_dim, 2, dtype=jnp.float32) / head_dim)
    angles = positions.astype(jnp.float32)[:, None] * inv_freq[None, :]
    return jnp.cos(angles), jnp.sin(angles)


def apply_rope(values, cos_tab, sin_tab):
    half_dim = values.shape[-1] // 2
    first_half = values[..., :half_dim]
    second_half = values[..., half_dim:]
    cos_rows = cos_tab[:, None, :]
    sin_rows = sin_tab[:, None, :]
    return jnp.concatenate([first_half * cos_rows - second_half * sin_rows, second_half * cos_rows + first_half * sin_rows], axis=-1)


def rms_norm(values, gain_vec):
    vals32 = values.astype(jnp.float32)
    inv_rms = lax.rsqrt(jnp.mean(vals32 * vals32, axis=-1, keepdims=True) + NORM_EPS)
    return (vals32 * inv_rms * gain_vec.astype(jnp.float32)).astype(jnp.bfloat16)


def flash_kernel(groups, key_rows, use_prefix, use_suffix, second_block, q_row0, has_state, *refs):
    refs = list(refs)
    q_ref = refs.pop(0)
    state_ref = refs.pop(0) if has_state else None
    n_parts = int(use_prefix) + int(use_suffix)
    n_slots = groups * n_parts
    per_part = groups + 2
    src_refs = [refs.pop(0) for _ in range(per_part * n_parts)]
    out_ref = refs.pop(0)
    kv_scr, s_scr, sems = refs
    head_dim = q_ref.shape[-1]
    tq = q_ref.shape[0]
    scale = (head_dim ** -0.5) * LOG2E
    group = pl.program_id(0)
    n_groups = kv_scr.shape[0]

    def copies(g):
        out = []
        for part in range(n_parts):
            for slot in range(groups):
                if slot < groups - 2:
                    src = src_refs[part * per_part + slot].at[g]
                else:
                    src = src_refs[part * per_part + groups - 2 + (slot - groups + 2) * 2 + g]
                dst_slot = part * groups + slot
                out.append(pltpu.make_async_copy(src, kv_scr.at[g, dst_slot], sems.at[g, dst_slot]))
        return out

    first = (pl.program_id(1) == 0) & (pl.program_id(2) == 0)

    @pl.when(first & (group == 0))
    def _():
        for g in range(n_groups):
            for cp in copies(g):
                cp.start()
        for cp in copies(0):
            cp.wait()

    for g in range(1, n_groups):
        @pl.when(first & (group == g))
        def _():
            for cp in copies(g):
                cp.wait()

    me = lax.axis_index('cp')
    my_x, my_core = me // 2, me % 2
    blk = (2 * groups - 1 - me) if second_block else me
    half = key_rows // 2
    q = q_ref[...]

    def locate(j):
        n_pre = 2 * groups if use_prefix else 0
        b = j - n_pre
        lower = b < groups
        dev = jnp.where(lower, b, 2 * groups - 1 - b)
        rel = (dev // 2 - my_x + groups // 2) % (groups // 2)
        order = jnp.where(rel == 0, 0, jnp.where(rel == 1, 2, jnp.where(rel == 2, 3, 1)))
        s_slot = order * 2 + jnp.where(dev % 2 == my_core, 0, 1) + (groups if use_prefix else 0)
        s_off = jnp.where(lower, 0, half)
        if not use_suffix:
            return j // 2, (j % 2) * half
        if not use_prefix:
            return s_slot, s_off
        pre = j < n_pre
        return jnp.where(pre, j // 2, s_slot), jnp.where(pre, (j % 2) * half, s_off)

    def scores(j):
        slot, off = locate(j)
        k = kv_scr[group, slot, pl.ds(pl.multiple_of(off, half), half), :]
        return lax.dot_general(k, q, (((1,), (1,)), ((), ())), preferred_element_type=jnp.float32)

    def values_t(j):
        slot, off = locate(j)
        v = kv_scr[group, slot, pl.ds(pl.multiple_of(key_rows + off, half), half), :]
        return jnp.concatenate([v[i * head_dim:(i + 1) * head_dim] for i in range(half // head_dim)], axis=1)

    def update(s, v, state):
        m, l, acc = state
        n = s.shape[0]
        folded = jnp.max(s.reshape(n // 8, 8, tq), axis=0)
        m_new = jnp.maximum(m, jnp.max(folded, axis=0, keepdims=True))
        a = jnp.exp2((m - m_new) * scale)
        p = jnp.exp2(s * scale - m_new * scale)
        l = l * a + jnp.sum(p.reshape(n // 8, 8, tq), axis=0)
        acc = acc * a + jnp.dot(v, p.astype(jnp.bfloat16), preferred_element_type=jnp.float32)
        return m_new, l, acc

    n_pre = 2 * groups if use_prefix else 0
    n_full = n_pre + (blk if use_suffix else 0)
    last = n_full if use_suffix else n_full - 1
    if has_state:
        st = state_ref[0]
        state = (st[head_dim + 8:head_dim + 9], st[head_dim:head_dim + 8], st[:head_dim])
    else:
        state = (jnp.full((1, tq), -jnp.inf, jnp.float32), jnp.zeros((8, tq), jnp.float32), jnp.zeros((head_dim, tq), jnp.float32))

    s_scr[0] = scores(0)

    def make_body(base, unroll):
        def body(i, st):
            for u in range(unroll):
                j = base + i * unroll + u
                s_scr[(u + 1) % 2] = scores(jnp.minimum(j + 1, last))
                st = update(s_scr[u % 2], values_t(j), st)
            return st
        return body

    if use_prefix:
        state = lax.fori_loop(0, n_pre // 4, make_body(0, 4), state)
    if use_suffix:
        state = lax.fori_loop(0, blk // 2, make_body(n_pre, 2), state)

        def odd_body(i, st):
            s_scr[1] = scores(last)
            return update(s_scr[0], values_t(last - 1), st)

        state = lax.fori_loop(0, blk % 2, odd_body, state)
        s = s_scr[blk % 2]
        kid = lax.broadcasted_iota(jnp.int32, s.shape, 0)
        qid = lax.broadcasted_iota(jnp.int32, s.shape, 1) + (q_row0 + pl.program_id(2) * tq) % half
        state = update(jnp.where(kid <= qid, s, -jnp.inf), values_t(last), state)
        m, l, acc = state
        out = acc / jnp.sum(l, axis=0, keepdims=True)
        out_ref[...] = out.T.astype(out_ref.dtype)
    else:
        m, l, acc = state
        out_ref[0, :head_dim] = acc
        out_ref[0, head_dim:head_dim + 8] = l
        out_ref[0, head_dim + 8:] = jnp.broadcast_to(m, (8, tq))


def flash(q, kv_parts, groups, kv_heads, head_dim, second_block, row0, rows, use_prefix, use_suffix, state=None, tq=512):
    heads = q.shape[1] // head_dim
    ratio = heads // kv_heads
    key_rows = kv_parts[0][0].shape[1] // 2
    tq = min(tq, rows)
    t0 = row0 // tq
    n_parts = len(kv_parts)
    q_spec = pl.BlockSpec((tq, head_dim), lambda g, r, t: (t0 + t, g * ratio + r))
    st_spec = pl.BlockSpec((1, head_dim + 16, tq), lambda g, r, t: (g * ratio + r, 0, t))
    flat = [a for part in kv_parts for a in part]
    args, specs = [q], [q_spec]
    if state is not None:
        args.append(state)
        specs.append(st_spec)
    args += flat
    specs += [pl.BlockSpec(memory_space=pl.ANY)] * len(flat)
    if use_suffix:
        out_shape = jax.ShapeDtypeStruct((rows, heads * head_dim), jnp.bfloat16)
        out_spec = pl.BlockSpec((tq, head_dim), lambda g, r, t: (t, g * ratio + r))
    else:
        out_shape = jax.ShapeDtypeStruct((heads, head_dim + 16, rows), jnp.float32)
        out_spec = st_spec
    n_keys = (2 * groups * use_prefix + (groups + groups // 2 if second_block else groups // 2) * use_suffix) * (key_rows // 2)
    return pl.pallas_call(
        functools.partial(flash_kernel, groups, key_rows, use_prefix, use_suffix, second_block, row0, state is not None),
        grid=(kv_heads, ratio, rows // tq),
        in_specs=specs,
        out_specs=out_spec,
        out_shape=out_shape,
        scratch_shapes=[
            pltpu.VMEM((kv_heads, groups * n_parts, 2 * key_rows, head_dim), jnp.bfloat16),
            pltpu.VMEM((2, key_rows // 2, tq), jnp.float32),
            pltpu.SemaphoreType.DMA((kv_heads, groups * n_parts)),
        ],
        compiler_params=pltpu.CompilerParams(vmem_limit_bytes=48 * 2**20, dimension_semantics=("arbitrary",) * 3),
        cost_estimate=pl.CostEstimate(flops=rows * heads * n_keys * 4 * head_dim, bytes_accessed=16 * 2**20, transcendentals=rows * heads * n_keys),
        name="flash",
    )(*args)


def solution(mesh):
    groups = mesh.shape['cp']
    tp = mesh.shape['tp']
    up = [(i, (i + 1) % tp) for i in range(tp)]
    down = [(i, (i - 1) % tp) for i in range(tp)]
    x_up = [(i, (i + 2) % groups) for i in range(groups)]
    x_down = [(i, (i - 2) % groups) for i in range(groups)]
    sibling = [(i, i ^ 1) for i in range(groups)]

    def ring_kv(bundle):
        r1 = lax.ppermute(bundle, 'cp', x_up)
        l1 = lax.ppermute(bundle, 'cp', x_down)
        own_s = lax.ppermute(bundle, 'cp', sibling)
        r2 = lax.ppermute(r1[0], 'cp', x_up)
        l2 = lax.ppermute(l1[1], 'cp', x_down)
        r1_s = lax.ppermute(r1, 'cp', sibling)
        l1_s = lax.ppermute(l1, 'cp', sibling)
        r2_s = lax.ppermute(r2, 'cp', sibling)
        l2_s = lax.ppermute(l2, 'cp', sibling)
        return [bundle, own_s, r1, r1_s, l1, l1_s, r2, l2, r2_s, l2_s]

    def tp_pieces(z):
        h = z.shape[0] // 2
        r1 = lax.ppermute(z, 'tp', up)
        l1 = lax.ppermute(z, 'tp', down)
        r2 = lax.ppermute(r1[:h], 'tp', up)
        l2 = lax.ppermute(l1[h:], 'tp', down)
        return r1, l1, r2, l2

    def local_layer(x_loc, kp_loc, vp_loc, norm_attn, w_query, w_key, w_value, w_out, norm_mlp, w_gate, w_up, w_down):
        rows_loc = x_loc.shape[0]
        blk_len = rows_loc // 2
        pre_dev, kv_loc, head_dim = kp_loc.shape
        heads_loc = w_query.shape[1] // head_dim
        prefix_len = pre_dev * groups
        my_cp = lax.axis_index('cp')
        my_tp = lax.axis_index('tp')

        def bundle_of(k, v):
            kt = jnp.moveaxis(k, 1, 0)
            vt = v.reshape(rows_loc // head_dim, head_dim, kv_loc, head_dim).transpose(2, 0, 3, 1).reshape(kv_loc, rows_loc, head_dim)
            return jnp.concatenate([kt, vt], axis=1)

        pre_slots = ring_kv(bundle_of(kp_loc, vp_loc))

        w_rows = w_out.shape[0] // groups
        w_out_full = lax.all_gather(lax.dynamic_slice_in_dim(w_out, my_cp * w_rows, w_rows, 0), ('tp', 'cp'), tiled=True)

        local_row = jnp.arange(rows_loc, dtype=jnp.int32)
        blk_idx = jnp.where(local_row < blk_len, my_cp, 2 * groups - 1 - my_cp)
        q_pos = prefix_len + blk_idx * blk_len + local_row % blk_len
        cos_tab, sin_tab = rope_tables(q_pos, head_dim)
        hidden = rms_norm(x_loc, norm_attn)
        k_proj = jnp.dot(hidden, w_key, preferred_element_type=jnp.float32).reshape(rows_loc, kv_loc, head_dim)
        k_new = apply_rope(k_proj, cos_tab, sin_tab).astype(jnp.bfloat16)
        v_new = jnp.dot(hidden, w_value, preferred_element_type=jnp.float32).astype(jnp.bfloat16).reshape(rows_loc, kv_loc, head_dim)
        suf_slots = ring_kv(bundle_of(k_new, v_new))
        q_proj = jnp.dot(hidden, w_query, preferred_element_type=jnp.float32).reshape(rows_loc, heads_loc, head_dim)
        q_rot = apply_rope(q_proj, cos_tab, sin_tab).astype(jnp.bfloat16).reshape(rows_loc, heads_loc * head_dim)

        fl = functools.partial(flash, groups=groups, kv_heads=kv_loc, head_dim=head_dim)
        st_a = fl(q_rot, [pre_slots], second_block=False, row0=0, rows=blk_len, use_prefix=True, use_suffix=False)
        o_a = fl(q_rot, [suf_slots], second_block=False, row0=0, rows=blk_len, use_prefix=False, use_suffix=True, state=st_a)
        q_b, o_a = lax.optimization_barrier((q_rot, o_a))
        o_b = fl(q_b, [pre_slots, suf_slots], second_block=True, row0=blk_len, rows=blk_len, use_prefix=True, use_suffix=True)

        def gather_heads(o):
            r1, l1, r2, l2 = tp_pieces(o)
            width = o.shape[1]
            far = jnp.concatenate([r2, l2], axis=0)
            full = jnp.zeros((o.shape[0], width * tp), o.dtype)
            for piece, off in ((o, 0), (r1, -1), (l1, 1), (far, 2)):
                full = lax.dynamic_update_slice(full, piece, (0, ((my_tp + off) % tp) * width))
            return full

        def mlp(x_rows, o_full):
            rows = x_rows.shape[0]
            shard = rows // tp
            h = shard // 2
            resid = x_rows.astype(jnp.float32) + jnp.dot(o_full, w_out_full, preferred_element_type=jnp.float32)
            hidden_mlp = rms_norm(resid, norm_mlp)
            gate_proj = jnp.dot(hidden_mlp, w_gate, preferred_element_type=jnp.float32)
            up_proj = jnp.dot(hidden_mlp, w_up, preferred_element_type=jnp.float32)
            act = (jax.nn.silu(gate_proj) * up_proj).astype(jnp.bfloat16)
            part = jnp.dot(act, w_down, preferred_element_type=jnp.float32)

            def rows_of(arr, off, lo, n):
                return lax.dynamic_slice_in_dim(arr, ((my_tp + off) % tp) * shard + lo, n, 0)

            far_r = lax.ppermute(rows_of(part, 2, 0, h), 'tp', up)
            far_l = lax.ppermute(rows_of(part, 2, h, h), 'tp', down)
            to_up = jnp.concatenate([rows_of(part, 1, 0, h) + far_r, rows_of(part, 1, h, h)], axis=0)
            to_down = jnp.concatenate([rows_of(part, -1, 0, h), rows_of(part, -1, h, h) + far_l], axis=0)
            from_down = lax.ppermute(to_up, 'tp', up)
            from_up = lax.ppermute(to_down, 'tp', down)
            mine = (rows_of(resid, 0, 0, shard) + (rows_of(part, 0, 0, shard) + from_down + from_up)).astype(jnp.bfloat16)
            r1, l1, r2, l2 = tp_pieces(mine)
            return [(mine, 0, 0), (r1, -1, 0), (l1, 1, 0), (r2, 2, 0), (l2, 2, h)], shard

        x_out = jnp.zeros(x_loc.shape, x_loc.dtype)
        for row0, o in ((0, o_a), (blk_len, o_b)):
            pieces, shard = mlp(x_loc[row0:row0 + o.shape[0]], gather_heads(o))
            for piece, off, lo in pieces:
                x_out = lax.dynamic_update_slice(x_out, piece, (row0 + ((my_tp + off) % tp) * shard + lo, 0))
        return x_out, k_new, v_new

    row_spec = P(('dp', 'cp'), None)
    kv_spec = P(('dp', 'cp'), 'tp', None)
    col_spec = P(None, 'tp')
    row_split = P('tp', None)
    vec_spec = P(None)
    return jax.shard_map(local_layer, mesh=mesh, in_specs=(row_spec, kv_spec, kv_spec, vec_spec, col_spec, col_spec, col_spec, row_split, vec_spec, col_spec, col_spec, row_split), out_specs=(row_spec, kv_spec, kv_spec), check_vma=False)
```

time: 1570 us -> 842 us (0.54)
  waiting for transfers between devices: 673 us -> 261 us
  matrix products: 584 us -> 211 us
  other arithmetic: 236 us -> 46.5 us
  Pallas kernels: 0 us -> 172 us
  starting transfers between devices: 1.34 us -> 49.7 us
  local copies, waits for them, and re-layouts: 53.6 us -> 76 us
    psum x2 -> x0, waiting for transfers between devices: 576 us -> none  [the longest x1 290 us: local_layer(): lax.psum(jnp.dot(attn_heads, w_out, preferred_element_type=jnp.float32),...]
    dot_general x20 -> x8, matrix products: 560 us -> 191 us  [the longest x2 51.9 us: mlp(): up_proj = jnp.dot(hidden_mlp, w_up, preferred_element_type=jnp.float32)]
    reduce_sum x8 -> x0, other arithmetic: 173 us -> none  [attend_step(): denom_sum = denom_sum * correction + jnp.sum(weights, axis=-1)]
    pallas_call x0 -> x3, Pallas kernels: none -> 172 us  [flash(): pl.pallas_call(functools.partial(flash_kernel, groups, key_rows, use_pref...]
    ppermute x14 -> x42, waiting for transfers between devices: 97 us -> 261 us  [the longest x4 63.2 us: tp_pieces(): r1 = lax.ppermute(z, 'tp', up)]
    ppermute x14 -> x42, starting transfers between devices: 1.21 us -> 49.6 us  [the longest x4 14.6 us: tp_pieces(): l2 = lax.ppermute(l1[h:], 'tp', down)]
    while x22 -> x0, local copies, waits for them, and re-layouts: 28 us -> none
    convert_element_type x3 -> x1, other arithmetic: 26.7 us -> 0.01 us  [rope_tables(): angles = positions.astype(jnp.float32)[:, None] * inv_freq[None, :]]
  transfers between devices with their start and end apart: 16 -> 43, of which waited for: 9 -> 16; matrix products, arithmetic and copies ran while one was open for 23% -> 23% of each run, Pallas kernels for 0% -> 21%
where the time goes in v1:
time: 842 us; the launch traced here: 831 us
  waiting for transfers between devices  261 us (31%)
  matrix products  211 us (25%)
  Pallas kernels  172 us (20%)
  local copies, waits for them, and re-layouts  76 us (9%)
  starting transfers between devices  49.7 us (6%)
  other arithmetic  46.5 us (6%)
  between operations  15.2 us (2%)
    pallas_call x3, Pallas kernels, flash(): pl.pallas_call(functools.partial(flash_kernel, groups, key_rows, use_pref...  172 us
    ppermute x4, waiting for transfers between devices, tp_pieces(): r1 = lax.ppermute(z, 'tp', up)  63.2 us
    ppermute x2, waiting for transfers between devices, ring_kv(): l1 = lax.ppermute(bundle, 'cp', x_down)  59.9 us
    dot_general x2, matrix products, mlp(): up_proj = jnp.dot(hidden_mlp, w_up, preferred_element_type=jnp.float32)  51.9 us
    dot_general x2, matrix products, mlp(): gate_proj = jnp.dot(hidden_mlp, w_gate, preferred_element_type=jnp.float32)  50.2 us
    dot_general x2, matrix products, mlp(): jnp.dot(o_full, w_out_full, preferred_element_type=jnp.float32)  49.1 us
    dot_general x2, matrix products, mlp(): part = jnp.dot(act, w_down, preferred_element_type=jnp.float32)  40 us
    ppermute x2, waiting for transfers between devices, mlp(): from_down = lax.ppermute(to_up, 'tp', up)  38.7 us
  transfers between devices with their start and end apart: 43, of which 16 were waited for; matrix products, arithmetic and copies ran while one was open for 23% of the time, Pallas kernels for 21%

profile of v1, /device:TPU:96, one launch (start us, length us, event | category | flops | bytes accessed | tf_op | source)
XLA Modules:
  0.0 831.2 jit_solution(3221183957561353689)
XLA Ops:
  10.6 5.2 fusion
  38.8 14.0 %fusion.19 = f32[1024,1024]{0,1:T(8,128)S(1)} fusion(bf16[4096,1024]{1,0:T(8,128)(2,1)} %param.16, bf16[1024,4096]{1,0:T(8,128)(2,1)} %param.12, f32[4096]{0:T(1024)S(1)} %convert_element_type.55, f32[1024]{0:T(1024)S(1)} %add_rsqrt_fusion), kind=kOutput, calls=%fused_computation.88 | convolution fusion | flops 8606711808 | bytes 20992000 | tf_op jit(solution)/shard_map/dot_general | solution.py:265
  52.8 18.0 %collective-permute-done.12.refs_6_.refs_15_ = bf16[2,2048,128]{2,1,0:T(8,128)(2,1)} collective-permute-done((bf16[2,2048,128]{2,1,0:T(8,128)(2,1)S(1)}, bf16[2,2048,128]{2,1,0:T(8,128)(2,1)}, u32[]{:S(2)}, u32[]{:S(2)}) %collective-permute-start.12) | collective-permute-done | bytes 1048608 | tf_op jit(solution)/shard_map/ppermute | solution.py:219
  73.8 41.9 %collective-permute-done.3.refs_5_ = bf16[2,2048,128]{2,1,0:T(8,128)(2,1)S(1)} collective-permute-done((bf16[2,2048,128]{2,1,0:T(8,128)(2,1)S(1)}, bf16[2,2048,128]{2,1,0:T(8,128)(2,1)S(1)}, u32[]{:S(2)}, u32[]{:S(2)}) %collective-permute-start.3) | collective-permute-done | bytes 1048608 | tf_op jit(solution)/shard_map/ppermute | solution.py:219
  131.4 6.8 collective-permute-done.15.refs_9_.refs_18_
  139.4 20.7 %collective-permute-done.6.refs_8_ = bf16[2048,128]{1,0:T(8,128)(2,1)} collective-permute-done((bf16[2048,128]{1,0:T(8,128)(2,1)}, bf16[2048,128]{1,0:T(8,128)(2,1)}, u32[]{:S(2)}, u32[]{:S(2)}) %collective-permute-start.6) | collective-permute-done | bytes 524320 | tf_op jit(solution)/shard_map/ppermute | solution.py:222
  160.6 4.3 subtract_convert_fusion
  170.0 53.1 %flash.3.refs_1_ = f32[8,144,512]{2,1,0:T(8,128)} custom-call(bf16[1024,1024]{1,0:T(8,128)(2,1)} %bitcast.57, bf16[2,2048,128]{2,1,0:T(8,128)(2,1)S(1)} %pad_maximum_fusion.5.refs_1_, bf16[2,2048,128]{2,1,0:T(8,128)(2,1)} %collective-permute-done.refs_2_, bf16[2,2048,128]{2,1,0:T(8,128)(2,1)S(1)} %collective-permute-done.1.refs_3_, ...), custom_call_target="tpu_custom_call" | custom-call | flops 17179869184 | bytes 16777216 | tf_op jit(solution)/shard_map/flash/pallas_call | solution.py:191
  225.2 10.0 %flash.4 = bf16[512,1024]{1,0:T(8,128)(2,1)S(1)} custom-call(bf16[1024,1024]{1,0:T(8,128)(2,1)} %bitcast.58, f32[8,144,512]{2,1,0:T(8,128)} %flash.3.refs_1_, bf16[2,2048,128]{2,1,0:T(8,128)(2,1)S(1)} %pad_maximum_fusion.6.refs_2_.refs_11_, bf16[2,2048,128]{2,1,0:T(8,128)(2,1)S(1)} %collective-permute-done.9.refs_3_.refs_12_, ...), custom_call_target="tpu_custom_call" | custom-call | flops 4294967296 | bytes 16777216 | tf_op jit(solution)/shard_map/flash/pallas_call | solution.py:191
  235.2 108.5 %flash.5 = bf16[512,1024]{1,0:T(8,128)(2,1)S(1)} custom-call(bf16[1024,1024]{1,0:T(8,128)(2,1)} %bitcast.59, bf16[2,2048,128]{2,1,0:T(8,128)(2,1)} %copy-done.3, bf16[2,2048,128]{2,1,0:T(8,128)(2,1)} %collective-permute-done.refs_2_, bf16[2,2048,128]{2,1,0:T(8,128)(2,1)} %copy-done.4, bf16[2,2048,128]{2,1,0:T(8,128)(2,1)} %copy-done.20, ...), custom_call_target="tpu_custom_call" | custom-call | flops 30064771072 | bytes 16777216 | tf_op jit(solution)/shard_map/flash/pallas_call | solution.py:191
  356.9 13.0 %collective-permute-done.31 = bf16[512,1024]{1,0:T(8,128)(2,1)S(1)} collective-permute-done((bf16[512,1024]{1,0:T(8,128)(2,1)S(1)}, bf16[512,1024]{1,0:T(8,128)(2,1)S(1)}, u32[]{:S(2)}, u32[]{:S(2)}) %collective-permute-start.31) | collective-permute-done | bytes 1048608 | tf_op jit(solution)/shard_map/ppermute | solution.py:232
  374.9 17.4 %collective-permute-done.19 = bf16[512,1024]{1,0:T(8,128)(2,1)} collective-permute-done((bf16[512,1024]{1,0:T(8,128)(2,1)S(1)}, bf16[512,1024]{1,0:T(8,128)(2,1)}, u32[]{:S(2)}, u32[]{:S(2)}) %collective-permute-start.19) | collective-permute-done | bytes 1048608 | tf_op jit(solution)/shard_map/ppermute | solution.py:232
  393.4 4.2 collective-permute-start.21
  407.3 5.8 collective-permute-done.21
  418.1 24.5 %multiply_reduce_fusion.1 = (f32[512]{0:T(512)S(1)}, f32[512,4096]{1,0:T(8,128)}) fusion(bf16[512,4096]{1,0:T(8,128)(2,1)} %get-tuple-element.39, bf16[4096,4096]{1,0:T(8,128)(2,1)} %all-gather.2.cloned.1.call-done, bf16[1024,4096]{1,0:T(8,128)(2,1)} %param.12), kind=kOutput, calls=%fused_computation.9 | convolution fusion | flops 17188257792 | bytes 50333696 | tf_op jit(solution)/shard_map/dot_general | solution.py:287
  442.6 24.6 %multiply_reduce_fusion = (f32[512]{0:T(512)S(1)}, f32[512,4096]{1,0:T(8,128)}) fusion(bf16[512,4096]{1,0:T(8,128)(2,1)} %get-tuple-element.40, bf16[4096,4096]{1,0:T(8,128)(2,1)} %all-gather.2.cloned.1.call-done, bf16[1024,4096]{1,0:T(8,128)(2,1)} %param.12), kind=kOutput, calls=%fused_computation.6 | convolution fusion | flops 17188257792 | bytes 50333696 | tf_op jit(solution)/shard_map/dot_general | solution.py:287
  467.2 25.0 %fusion.14 = f32[512,3584]{1,0:T(8,128)} fusion(bf16[4096,3584]{1,0:T(8,128)(2,1)} %param.21, f32[512,4096]{1,0:T(8,128)} %get-tuple-element.36, f32[4096]{0:T(1024)S(1)} %convert_element_type.60, f32[512]{0:T(512)S(1)} %add_rsqrt_fusion.2), kind=kOutput, calls=%fused_computation.85 | convolution fusion | flops 15038676992 | bytes 45107200 | tf_op jit(solution)/shard_map/dot_general | solution.py:289
  492.2 26.0 %multiply_convert_fusion.3.clone.4 = bf16[512,3584]{1,0:T(8,128)(2,1)} fusion(f32[512,3584]{1,0:T(8,128)} %fusion.14, bf16[4096,3584]{1,0:T(8,128)(2,1)} %param.22, f32[512,4096]{1,0:T(8,128)} %get-tuple-element.36, f32[4096]{0:T(1024)S(1)} %convert_element_type.60, f32[512]{0:T(512)S(1)} %add_rsqrt_fusion.2), kind=kOutput, calls=%fused_computation.12.clone.clone.clone.1 | convolution fusion | flops 15049687040 | bytes 48777216 | tf_op jit(solution)/shard_map/dot_general | solution.py:290
  518.2 20.0 %fusion.4 = f32[512,4096]{1,0:T(8,128)S(1)} fusion(bf16[3584,4096]{1,0:T(8,128)(2,1)} %param.23, bf16[512,3584]{1,0:T(8,128)(2,1)} %multiply_convert_fusion.3.clone.4), kind=kOutput, calls=%fused_computation.14 | convolution fusion | flops 15032385536 | bytes 41418752 | tf_op jit(solution)/shard_map/dot_general | solution.py:292
  541.7 25.2 %fusion.15 = f32[512,3584]{1,0:T(8,128)} fusion(bf16[4096,3584]{1,0:T(8,128)(2,1)} %param.21, f32[512,4096]{1,0:T(8,128)} %get-tuple-element.38, f32[512]{0:T(512)S(1)} %add_rsqrt_fusion.1, f32[4096]{0:T(1024)S(1)} %convert_element_type.60), kind=kOutput, calls=%fused_computation.86 | convolution fusion | flops 15038676992 | bytes 45107200 | tf_op jit(solution)/shard_map/dot_general | solution.py:289
  566.9 25.9 %multiply_convert_fusion.2.clone.4 = bf16[512,3584]{1,0:T(8,128)(2,1)} fusion(f32[512,3584]{1,0:T(8,128)} %fusion.15, bf16[4096,3584]{1,0:T(8,128)(2,1)} %param.22, f32[512,4096]{1,0:T(8,128)} %get-tuple-element.38, f32[512]{0:T(512)S(1)} %add_rsqrt_fusion.1, f32[4096]{0:T(1024)S(1)} %convert_element_type.60), kind=kOutput, calls=%fused_computation.11.clone.clone.clone.1 | convolution fusion | flops 15049687040 | bytes 48777216 | tf_op jit(solution)/shard_map/dot_general | solution.py:290
  592.8 4.0 dynamic-slice_add_fusion.3
  600.0 20.0 %fusion.3 = f32[512,4096]{1,0:T(8,128)S(1)} fusion(bf16[3584,4096]{1,0:T(8,128)(2,1)} %param.23, bf16[512,3584]{1,0:T(8,128)(2,1)} %multiply_convert_fusion.2.clone.4), kind=kOutput, calls=%fused_computation.13 | convolution fusion | flops 15032385536 | bytes 41418752 | tf_op jit(solution)/shard_map/dot_general | solution.py:292
  633.9 18.1 %collective-permute-done.34 = f32[64,4096]{1,0:T(8,128)S(1)} collective-permute-done((f32[64,4096]{1,0:T(8,128)}, f32[64,4096]{1,0:T(8,128)S(1)}, u32[]{:S(2)}, u32[]{:S(2)}) %collective-permute-start.34) | collective-permute-done | bytes 1048608 | tf_op jit(solution)/shard_map/ppermute | solution.py:297
  658.2 38.7 %collective-permute-done.23 = f32[128,4096]{1,0:T(8,128)} collective-permute-done((f32[128,4096]{1,0:T(8,128)}, f32[128,4096]{1,0:T(8,128)}, u32[]{:S(2)}, u32[]{:S(2)}) %collective-permute-start.23) | collective-permute-done | bytes 2097184 | tf_op jit(solution)/shard_map/ppermute | solution.py:301
  696.9 4.4 broadcast_in_dim.10
  701.3 5.3 constant_dynamic-update-slice_fusion.12
  712.9 48.0 %collective-permute-done.26 = bf16[128,4096]{1,0:T(8,128)(2,1)S(1)} collective-permute-done((bf16[128,4096]{1,0:T(8,128)(2,1)}, bf16[128,4096]{1,0:T(8,128)(2,1)S(1)}, u32[]{:S(2)}, u32[]{:S(2)}) %collective-permute-start.26) | collective-permute-done | bytes 1048608 | tf_op jit(solution)/shard_map/ppermute | solution.py:231
  768.7 4.0 collective-permute-done.28
  773.6 8.2 collective-permute-done.29
  782.6 5.5 constant_dynamic-update-slice_fusion.3
  795.5 15.2 %collective-permute-done.38 = bf16[128,4096]{1,0:T(8,128)(2,1)} collective-permute-done((bf16[128,4096]{1,0:T(8,128)(2,1)}, bf16[128,4096]{1,0:T(8,128)(2,1)}, u32[]{:S(2)}, u32[]{:S(2)}) %collective-permute-start.38) | collective-permute-done | bytes 1048608 | tf_op jit(solution)/shard_map/ppermute | solution.py:231
  (187 shorter events, 150.4 us)
Async XLA Ops:
  7.2 410.9 %all-gather.2.cloned.1.call-start = ((), (), s32[]{:S(2)}) async-start(), calls=%async_computation | async-start | bytes 34603008 | tf_op jit(solution)/shard_map/all_gather | solution.py:254
  29.8 41.0 %collective-permute-start.12 = (bf16[2,2048,128]{2,1,0:T(8,128)(2,1)S(1)}, bf16[2,2048,128]{2,1,0:T(8,128)(2,1)}, u32[]{:S(2)}, u32[]{:S(2)}) collective-permute-start(bf16[2,2048,128]{2,1,0:T(8,128)(2,1)S(1)} %pad_maximum_fusion.6.refs_2_.refs_11_), channel_id=1, source_target_pairs={{0,6},{1,7},{2,0},{3,1},{4,2},{5,3},{6,4},{7,5},{8,14},{9,15},{10,... | collective-permute-start | bytes 3145736 | tf_op jit(solution)/shard_map/ppermute | solution.py:219
  32.5 97.3 %collective-permute-start.10 = (bf16[2,2048,128]{2,1,0:T(8,128)(2,1)S(1)}, bf16[2,2048,128]{2,1,0:T(8,128)(2,1)}, u32[]{:S(2)}, u32[]{:S(2)}) collective-permute-start(bf16[2,2048,128]{2,1,0:T(8,128)(2,1)S(1)} %pad_maximum_fusion.6.refs_2_.refs_11_), channel_id=1, source_target_pairs={{0,2},{1,3},{2,4},{3,5},{4,6},{5,7},{6,0},{7,1},{8,10},{9,11},{10,... | collective-permute-start | bytes 3145736 | tf_op jit(solution)/shard_map/ppermute | solution.py:218
  35.1 80.7 %collective-permute-start.3 = (bf16[2,2048,128]{2,1,0:T(8,128)(2,1)S(1)}, bf16[2,2048,128]{2,1,0:T(8,128)(2,1)S(1)}, u32[]{:S(2)}, u32[]{:S(2)}) collective-permute-start(bf16[2,2048,128]{2,1,0:T(8,128)(2,1)S(1)} %pad_maximum_fusion.5.refs_1_), channel_id=1, source_target_pairs={{0,6},{1,7},{2,0},{3,1},{4,2},{5,3},{6,4},{7,5},{8,14},{9,15},{10,... | collective-permute-start | bytes 3145736 | tf_op jit(solution)/shard_map/ppermute | solution.py:219
  38.4 79.4 %collective-permute-start.1 = (bf16[2,2048,128]{2,1,0:T(8,128)(2,1)S(1)}, bf16[2,2048,128]{2,1,0:T(8,128)(2,1)S(1)}, u32[]{:S(2)}, u32[]{:S(2)}) collective-permute-start(bf16[2,2048,128]{2,1,0:T(8,128)(2,1)S(1)} %pad_maximum_fusion.5.refs_1_), channel_id=1, source_target_pairs={{0,2},{1,3},{2,4},{3,5},{4,6},{5,7},{6,0},{7,1},{8,10},{9,11},{10,... | collective-permute-start | bytes 3145736 | tf_op jit(solution)/shard_map/ppermute | solution.py:218
  38.6 91.2 %collective-permute-start = (bf16[2,2048,128]{2,1,0:T(8,128)(2,1)S(1)}, bf16[2,2048,128]{2,1,0:T(8,128)(2,1)}, u32[]{:S(2)}, u32[]{:S(2)}) collective-permute-start(bf16[2,2048,128]{2,1,0:T(8,128)(2,1)S(1)} %pad_maximum_fusion.5.refs_1_), channel_id=1, source_target_pairs={{0,1},{1,0},{2,3},{3,2},{4,5},{5,4},{6,7},{7,6},{8,9},{9,8},{10,11... | collective-permute-start | bytes 3145736 | tf_op jit(solution)/shard_map/ppermute | solution.py:220
  72.7 65.5 %collective-permute-start.15 = (bf16[2048,128]{1,0:T(8,128)(2,1)}, bf16[2048,128]{1,0:T(8,128)(2,1)}, u32[]{:S(2)}, u32[]{:S(2)}) collective-permute-start(bf16[2048,128]{1,0:T(8,128)(2,1)} %slice_bitcast_fusion), channel_id=1, source_target_pairs={{0,6},{1,7},{2,0},{3,1},{4,2},{5,3},{6,4},{7,5},{8,14},{9,15},{10,... | collective-permute-start | bytes 1572872 | tf_op jit(solution)/shard_map/ppermute | solution.py:222
  116.6 43.5 %collective-permute-start.6 = (bf16[2048,128]{1,0:T(8,128)(2,1)}, bf16[2048,128]{1,0:T(8,128)(2,1)}, u32[]{:S(2)}, u32[]{:S(2)}) collective-permute-start(bf16[2048,128]{1,0:T(8,128)(2,1)} %slice_bitcast_fusion.2), channel_id=1, source_target_pairs={{0,6},{1,7},{2,0},{3,1},{4,2},{5,3},{6,4},{7,5},{8,14},{9,15},{10,... | collective-permute-start | bytes 1572872 | tf_op jit(solution)/shard_map/ppermute | solution.py:222
  118.6 41.4 %collective-permute-start.5 = (bf16[2048,128]{1,0:T(8,128)(2,1)}, bf16[2048,128]{1,0:T(8,128)(2,1)}, u32[]{:S(2)}, u32[]{:S(2)}) collective-permute-start(bf16[2048,128]{1,0:T(8,128)(2,1)} %slice_bitcast_fusion.3), channel_id=1, source_target_pairs={{0,2},{1,3},{2,4},{3,5},{4,6},{5,7},{6,0},{7,1},{8,10},{9,11},{10,... | collective-permute-start | bytes 1572872 | tf_op jit(solution)/shard_map/ppermute | solution.py:221
  129.8 38.7 %collective-permute-start.4 = (bf16[2,2048,128]{2,1,0:T(8,128)(2,1)}, bf16[2,2048,128]{2,1,0:T(8,128)(2,1)S(1)}, u32[]{:S(2)}, u32[]{:S(2)}) collective-permute-start(bf16[2,2048,128]{2,1,0:T(8,128)(2,1)} %copy-done.16), channel_id=1, source_target_pairs={{0,1},{1,0},{2,3},{3,2},{4,5},{5,4},{6,7},{7,6},{8,9},{9,8},{10,11... | collective-permute-start | bytes 3145736 | tf_op jit(solution)/shard_map/ppermute | solution.py:224
  129.8 39.2 %collective-permute-start.2 = (bf16[2,2048,128]{2,1,0:T(8,128)(2,1)S(1)}, bf16[2,2048,128]{2,1,0:T(8,128)(2,1)S(1)}, u32[]{:S(2)}, u32[]{:S(2)}) collective-permute-start(bf16[2,2048,128]{2,1,0:T(8,128)(2,1)S(1)} %collective-permute-done.1.refs_3_), channel_id=1, source_target_pairs={{0,1},{1,0},{2,3},{3,2},{4,5},{5,4},{6,7},{7,6},{8,9},{9,8},{10,11... | collective-permute-start | bytes 3145736 | tf_op jit(solution)/shard_map/ppermute | solution.py:223
  138.2 29.8 %collective-permute-start.14 = (bf16[2048,128]{1,0:T(8,128)(2,1)S(1)}, bf16[2048,128]{1,0:T(8,128)(2,1)S(1)}, u32[]{:S(2)}, u32[]{:S(2)}) collective-permute-start(bf16[2048,128]{1,0:T(8,128)(2,1)S(1)} %slice_bitcast_fusion.1), channel_id=1, source_target_pairs={{0,2},{1,3},{2,4},{3,5},{4,6},{5,7},{6,0},{7,1},{8,10},{9,11},{10,... | collective-permute-start | bytes 1572872 | tf_op jit(solution)/shard_map/ppermute | solution.py:221
  168.0 55.2 %collective-permute-start.9 = (bf16[2,2048,128]{2,1,0:T(8,128)(2,1)S(1)}, bf16[2,2048,128]{2,1,0:T(8,128)(2,1)S(1)}, u32[]{:S(2)}, u32[]{:S(2)}) collective-permute-start(bf16[2,2048,128]{2,1,0:T(8,128)(2,1)S(1)} %pad_maximum_fusion.6.refs_2_.refs_11_), channel_id=1, source_target_pairs={{0,1},{1,0},{2,3},{3,2},{4,5},{5,4},{6,7},{7,6},{8,9},{9,8},{10,11... | collective-permute-start | bytes 3145736 | tf_op jit(solution)/shard_map/ppermute | solution.py:220
  168.0 55.2 %collective-permute-start.13 = (bf16[2,2048,128]{2,1,0:T(8,128)(2,1)}, bf16[2,2048,128]{2,1,0:T(8,128)(2,1)S(1)}, u32[]{:S(2)}, u32[]{:S(2)}) collective-permute-start(bf16[2,2048,128]{2,1,0:T(8,128)(2,1)} %collective-permute-done.12.refs_6_.refs_15_), channel_id=1, source_target_pairs={{0,1},{1,0},{2,3},{3,2},{4,5},{5,4},{6,7},{7,6},{8,9},{9,8},{10,11... | collective-permute-start | bytes 3145736 | tf_op jit(solution)/shard_map/ppermute | solution.py:224
  168.5 54.7 %collective-permute-start.11 = (bf16[2,2048,128]{2,1,0:T(8,128)(2,1)}, bf16[2,2048,128]{2,1,0:T(8,128)(2,1)S(1)}, u32[]{:S(2)}, u32[]{:S(2)}) collective-permute-start(bf16[2,2048,128]{2,1,0:T(8,128)(2,1)} %collective-permute-done.10.refs_4_.refs_13_), channel_id=1, source_target_pairs={{0,1},{1,0},{2,3},{3,2},{4,5},{5,4},{6,7},{7,6},{8,9},{9,8},{10,11... | collective-permute-start | bytes 3145736 | tf_op jit(solution)/shard_map/ppermute | solution.py:223
  168.6 54.6 %collective-permute-start.17 = (bf16[2048,128]{1,0:T(8,128)(2,1)}, bf16[2048,128]{1,0:T(8,128)(2,1)S(1)}, u32[]{:S(2)}, u32[]{:S(2)}) collective-permute-start(bf16[2048,128]{1,0:T(8,128)(2,1)} %collective-permute-done.15.refs_9_.refs_18_), channel_id=1, source_target_pairs={{0,1},{1,0},{2,3},{3,2},{4,5},{5,4},{6,7},{7,6},{8,9},{9,8},{10,11... | collective-permute-start | bytes 1572872 | tf_op jit(solution)/shard_map/ppermute | solution.py:226
  169.0 54.2 %collective-permute-start.16 = (bf16[2048,128]{1,0:T(8,128)(2,1)S(1)}, bf16[2048,128]{1,0:T(8,128)(2,1)S(1)}, u32[]{:S(2)}, u32[]{:S(2)}) collective-permute-start(bf16[2048,128]{1,0:T(8,128)(2,1)S(1)} %collective-permute-done.14.refs_8_.refs_17_), channel_id=1, source_target_pairs={{0,1},{1,0},{2,3},{3,2},{4,5},{5,4},{6,7},{7,6},{8,9},{9,8},{10,11... | collective-permute-start | bytes 1572872 | tf_op jit(solution)/shard_map/ppermute | solution.py:225
  346.4 27.4 %collective-permute-start.30 = (bf16[512,1024]{1,0:T(8,128)(2,1)S(1)}, bf16[512,1024]{1,0:T(8,128)(2,1)}, u32[]{:S(2)}, u32[]{:S(2)}) collective-permute-start(bf16[512,1024]{1,0:T(8,128)(2,1)S(1)} %flash.5), channel_id=1, source_target_pairs={{0,8},{8,16},{16,24},{24,0},{1,9},{9,17},{17,25},{25,1},{2,10},{10... | collective-permute-start | bytes 3145736 | tf_op jit(solution)/shard_map/ppermute | solution.py:231
  346.4 46.0 %collective-permute-start.19 = (bf16[512,1024]{1,0:T(8,128)(2,1)S(1)}, bf16[512,1024]{1,0:T(8,128)(2,1)}, u32[]{:S(2)}, u32[]{:S(2)}) collective-permute-start(bf16[512,1024]{1,0:T(8,128)(2,1)S(1)} %flash.4), channel_id=1, source_target_pairs={{0,24},{8,0},{16,8},{24,16},{1,25},{9,1},{17,9},{25,17},{2,26},{10... | collective-permute-start | bytes 3145736 | tf_op jit(solution)/shard_map/ppermute | solution.py:232
  349.6 48.1 %collective-permute-start.18 = (bf16[512,1024]{1,0:T(8,128)(2,1)S(1)}, bf16[512,1024]{1,0:T(8,128)(2,1)}, u32[]{:S(2)}, u32[]{:S(2)}) collective-permute-start(bf16[512,1024]{1,0:T(8,128)(2,1)S(1)} %flash.4), channel_id=1, source_target_pairs={{0,8},{8,16},{16,24},{24,0},{1,9},{9,17},{17,25},{25,1},{2,10},{10... | collective-permute-start | bytes 3145736 | tf_op jit(solution)/shard_map/ppermute | solution.py:231
  369.9 36.9 %collective-permute-start.33 = (bf16[256,1024]{1,0:T(8,128)(2,1)S(1)}, bf16[256,1024]{1,0:T(8,128)(2,1)S(1)}, u32[]{:S(2)}, u32[]{:S(2)}) collective-permute-start(bf16[256,1024]{1,0:T(8,128)(2,1)S(1)} %slice.85), channel_id=1, source_target_pairs={{0,24},{8,0},{16,8},{24,16},{1,25},{9,1},{17,9},{25,17},{2,26},{10... | collective-permute-start | bytes 1572872 | tf_op jit(solution)/shard_map/ppermute | solution.py:234
  374.8 32.5 %collective-permute-start.32 = (bf16[256,1024]{1,0:T(8,128)(2,1)S(1)}, bf16[256,1024]{1,0:T(8,128)(2,1)S(1)}, u32[]{:S(2)}, u32[]{:S(2)}) collective-permute-start(bf16[256,1024]{1,0:T(8,128)(2,1)S(1)} %slice.84), channel_id=1, source_target_pairs={{0,8},{8,16},{16,24},{24,0},{1,9},{9,17},{17,25},{25,1},{2,10},{10... | collective-permute-start | bytes 1572872 | tf_op jit(solution)/shard_map/ppermute | solution.py:233
  541.6 51.2 %collective-permute-start.22 = (f32[64,4096]{1,0:T(8,128)S(1)}, f32[64,4096]{1,0:T(8,128)S(1)}, u32[]{:S(2)}, u32[]{:S(2)}) collective-permute-start(f32[64,4096]{1,0:T(8,128)S(1)} %constant_dynamic-slice_fusion.7), channel_id=1, source_target_pairs={{0,8},{8,16},{16,24},{24,0},{1,9},{9,17},{17,25},{25,1},{2,10},{10... | collective-permute-start | bytes 3145736 | tf_op jit(solution)/shard_map/ppermute | solution.py:297
  596.9 30.6 %collective-permute-start.24 = (f32[64,4096]{1,0:T(8,128)}, f32[64,4096]{1,0:T(8,128)}, u32[]{:S(2)}, u32[]{:S(2)}) collective-permute-start(f32[64,4096]{1,0:T(8,128)} %get-tuple-element.24), channel_id=1, source_target_pairs={{0,24},{8,0},{16,8},{24,16},{1,25},{9,1},{17,9},{25,17},{2,26},{10... | collective-permute-start | bytes 3145736 | tf_op jit(solution)/shard_map/ppermute | solution.py:298
  624.5 27.5 %collective-permute-start.34 = (f32[64,4096]{1,0:T(8,128)}, f32[64,4096]{1,0:T(8,128)S(1)}, u32[]{:S(2)}, u32[]{:S(2)}) collective-permute-start(f32[64,4096]{1,0:T(8,128)} %constant_dynamic-slice_fusion.3), channel_id=1, source_target_pairs={{0,8},{8,16},{16,24},{24,0},{1,9},{9,17},{17,25},{25,1},{2,10},{10... | collective-permute-start | bytes 3145736 | tf_op jit(solution)/shard_map/ppermute | solution.py:297
  627.5 69.4 %collective-permute-start.23 = (f32[128,4096]{1,0:T(8,128)}, f32[128,4096]{1,0:T(8,128)}, u32[]{:S(2)}, u32[]{:S(2)}) collective-permute-start(f32[128,4096]{1,0:T(8,128)} %pad_maximum_fusion.1), channel_id=1, source_target_pairs={{0,8},{8,16},{16,24},{24,0},{1,9},{9,17},{17,25},{25,1},{2,10},{10... | collective-permute-start | bytes 6291464 | tf_op jit(solution)/shard_map/ppermute | solution.py:301
  630.6 66.2 %collective-permute-start.25 = (f32[128,4096]{1,0:T(8,128)}, f32[128,4096]{1,0:T(8,128)}, u32[]{:S(2)}, u32[]{:S(2)}) collective-permute-start(f32[128,4096]{1,0:T(8,128)} %pad_maximum_fusion.2), channel_id=1, source_target_pairs={{0,24},{8,0},{16,8},{24,16},{1,25},{9,1},{17,9},{25,17},{2,26},{10... | collective-permute-start | bytes 6291464 | tf_op jit(solution)/shard_map/ppermute | solution.py:302
  654.5 55.4 %collective-permute-start.36 = (f32[64,4096]{1,0:T(8,128)S(1)}, f32[64,4096]{1,0:T(8,128)S(1)}, u32[]{:S(2)}, u32[]{:S(2)}) collective-permute-start(f32[64,4096]{1,0:T(8,128)S(1)} %get-tuple-element.20), channel_id=1, source_target_pairs={{0,24},{8,0},{16,8},{24,16},{1,25},{9,1},{17,9},{25,17},{2,26},{10... | collective-permute-start | bytes 3145736 | tf_op jit(solution)/shard_map/ppermute | solution.py:298
  656.2 126.4 %collective-permute-start.35 = (f32[128,4096]{1,0:T(8,128)}, f32[128,4096]{1,0:T(8,128)}, u32[]{:S(2)}, u32[]{:S(2)}) collective-permute-start(f32[128,4096]{1,0:T(8,128)} %pad_maximum_fusion.3), channel_id=1, source_target_pairs={{0,8},{8,16},{16,24},{24,0},{1,9},{9,17},{17,25},{25,1},{2,10},{10... | collective-permute-start | bytes 6291464 | tf_op jit(solution)/shard_map/ppermute | solution.py:301
  706.7 54.2 %collective-permute-start.26 = (bf16[128,4096]{1,0:T(8,128)(2,1)}, bf16[128,4096]{1,0:T(8,128)(2,1)S(1)}, u32[]{:S(2)}, u32[]{:S(2)}) collective-permute-start(bf16[128,4096]{1,0:T(8,128)(2,1)} %get-tuple-element.16), channel_id=1, source_target_pairs={{0,8},{8,16},{16,24},{24,0},{1,9},{9,17},{17,25},{25,1},{2,10},{10... | collective-permute-start | bytes 3145736 | tf_op jit(solution)/shard_map/ppermute | solution.py:231
  706.7 54.4 %collective-permute-start.27 = (bf16[128,4096]{1,0:T(8,128)(2,1)}, bf16[128,4096]{1,0:T(8,128)(2,1)}, u32[]{:S(2)}, u32[]{:S(2)}) collective-permute-start(bf16[128,4096]{1,0:T(8,128)(2,1)} %get-tuple-element.16), channel_id=1, source_target_pairs={{0,24},{8,0},{16,8},{24,16},{1,25},{9,1},{17,9},{25,17},{2,26},{10... | collective-permute-start | bytes 3145736 | tf_op jit(solution)/shard_map/ppermute | solution.py:232
  712.9 69.7 %collective-permute-start.37 = (f32[128,4096]{1,0:T(8,128)}, f32[128,4096]{1,0:T(8,128)}, u32[]{:S(2)}, u32[]{:S(2)}) collective-permute-start(f32[128,4096]{1,0:T(8,128)} %pad_maximum_fusion.4), channel_id=1, source_target_pairs={{0,24},{8,0},{16,8},{24,16},{1,25},{9,1},{17,9},{25,17},{2,26},{10... | collective-permute-start | bytes 6291464 | tf_op jit(solution)/shard_map/ppermute | solution.py:302
  (34 other events, 832.4 us)
Sparse Core Ops, SparseCore 0:
  10.1 167.8 all-gather.1

commit v2 on v0

v2 whole, which is shorter than its diff:
```python
import functools

import jax
import jax.numpy as jnp
from jax import lax
from jax.experimental import pallas as pl
from jax.experimental.pallas import tpu as pltpu
from jax.sharding import PartitionSpec as P

ROPE_THETA = 500000.0
NORM_EPS = 1e-5
LOG2E = 1.4426950408889634
KEY_BLOCK = 512


def rope_tables(positions, head_dim):
    inv_freq = ROPE_THETA ** (-jnp.arange(0, head_dim, 2, dtype=jnp.float32) / head_dim)
    angles = positions.astype(jnp.float32)[:, None] * inv_freq[None, :]
    return jnp.cos(angles), jnp.sin(angles)


def apply_rope(values, cos_tab, sin_tab):
    half_dim = values.shape[-1] // 2
    first_half = values[..., :half_dim]
    second_half = values[..., half_dim:]
    cos_rows = cos_tab[:, None, :]
    sin_rows = sin_tab[:, None, :]
    return jnp.concatenate([first_half * cos_rows - second_half * sin_rows, second_half * cos_rows + first_half * sin_rows], axis=-1)


def rms_norm(values, gain_vec):
    vals32 = values.astype(jnp.float32)
    inv_rms = lax.rsqrt(jnp.mean(vals32 * vals32, axis=-1, keepdims=True) + NORM_EPS)
    return (vals32 * inv_rms * gain_vec.astype(jnp.float32)).astype(jnp.bfloat16)


def attn_kernel(cfg, *refs):
    groups, tp, kv_heads, ratio, head_dim, key_rows, rows, ring, upper = (
        cfg[k] for k in ('groups', 'tp', 'kv_heads', 'ratio', 'head_dim', 'key_rows', 'rows', 'ring', 'upper'))
    heads = kv_heads * ratio
    if ring:
        q_ref, pre_ref, suf_ref, o_full, kv_out, kv_scr, s_scr, o_scr, st_scr, kv_send, kv_recv, kv_save, o_send, o_recv, o_local = refs
    else:
        q_ref, kv_in, o_full, kv_scr, s_scr, o_scr, kv_recv, o_send, o_recv, o_local = refs
    me, my_tp = lax.axis_index('cp'), lax.axis_index('tp')
    my_x, my_core = me // 2, me % 2
    half = key_rows // 2
    scale = (head_dim ** -0.5) * LOG2E
    MESH = pl.DeviceIdType.MESH
    sib = {'cp': my_x * 2 + (1 - my_core)}
    x_next = {'cp': (me + 2) % groups}
    x_prev = {'cp': (me + groups - 2) % groups}
    peers = [{'tp': (my_tp + k) % tp} for k in range(1, tp)]

    barrier = pltpu.get_barrier_semaphore()
    greet = peers + ([sib, x_next, x_prev] if ring else [])
    for dev in greet:
        pl.semaphore_signal(barrier, inc=1, device_id=dev, device_id_type=MESH)
    pl.semaphore_wait(barrier, len(greet))

    def kv_copy(part, g, slot):
        base = part * groups
        src_own = (pre_ref, suf_ref)[part].at[g] if ring else None
        dst = kv_scr.at[g, base + slot]
        if slot == 0:
            return pltpu.make_async_copy(src_own, dst, kv_recv.at[g, base])
        if slot in (1, 2, 3):
            src = src_own
        elif slot in (4, 5):
            src = kv_scr.at[g, base + slot - 2]
        elif slot == 6:
            src = kv_scr.at[g, base + (2 if g == 0 else 3)]
        else:
            src = kv_scr.at[g, base + 6]
        dev = {1: sib, 4: sib, 5: sib, 7: sib, 2: x_next, 3: x_prev, 6: x_next if g == 0 else x_prev}[slot]
        return pltpu.make_async_remote_copy(src_ref=src, dst_ref=dst, send_sem=kv_send.at[g, base + slot], recv_sem=kv_recv.at[g, base + slot], device_id=dev, device_id_type=MESH)

    gs = range(kv_heads)

    def start(part, slots):
        for slot in slots:
            for g in gs:
                kv_copy(part, g, slot).start()

    def arrived(part, slots):
        for slot in slots:
            for g in gs:
                copy = kv_copy(part, g, slot)
                copy.wait() if slot == 0 else copy.wait_recv()

    blk = (2 * groups - 1 - me) if upper else me
    n_pre = 2 * groups

    def locate(j):
        b = j - n_pre
        lower = b < groups
        dev = jnp.where(lower, b, 2 * groups - 1 - b)
        rel = (dev // 2 - my_x + groups // 2) % (groups // 2)
        same = dev % 2 == my_core
        s_slot = jnp.where(rel == 0, jnp.where(same, 0, 1), jnp.where(rel == 1, jnp.where(same, 3, 5), jnp.where(rel == 2, jnp.where(same, 6, 7), jnp.where(same, 2, 4))))
        pre = j < n_pre
        return jnp.where(pre, j // 2, groups + s_slot), jnp.where(pre, (j % 2) * half, jnp.where(lower, 0, half))

    def head_pass(h, lo, hi, suffix, load, store):
        g = h // ratio
        q = q_ref[:, pl.ds(pl.multiple_of(h * head_dim, head_dim), head_dim)]

        def scores(j):
            slot, off = locate(j)
            k = kv_scr[g, slot, pl.ds(pl.multiple_of(off, half), half), :]
            return lax.dot_general(k, q, (((1,), (1,)), ((), ())), preferred_element_type=jnp.float32)

        def values_t(j):
            slot, off = locate(j)
            v = kv_scr[g, slot, pl.ds(pl.multiple_of(key_rows + off, half), half), :]
            return jnp.concatenate([v[i * head_dim:(i + 1) * head_dim] for i in range(half // head_dim)], axis=1)

        def update(s, v, state):
            m, l, acc = state
            n = s.shape[0]
            folded = jnp.max(s.reshape(n // 8, 8, rows), axis=0)
            m_new = jnp.maximum(m, jnp.max(folded, axis=0, keepdims=True))
            a = jnp.exp2((m - m_new) * scale)
            p = jnp.exp2(s * scale - m_new * scale)
            l = l * a + jnp.sum(p.reshape(n // 8, 8, rows), axis=0)
            acc = acc * a + jnp.dot(v, p.astype(jnp.bfloat16), preferred_element_type=jnp.float32)
            return m_new, l, acc

        last = n_pre + blk if suffix else hi - 1
        if load:
            state = (st_scr[h, head_dim + 8:head_dim + 9], st_scr[h, head_dim:head_dim + 8], st_scr[h, :head_dim])
        else:
            state = (jnp.full((1, rows), -jnp.inf, jnp.float32), jnp.zeros((8, rows), jnp.float32), jnp.zeros((head_dim, rows), jnp.float32))
        s_scr[0] = scores(lo)

        def make_body(base, unroll):
            def body(i, st):
                for u in range(unroll):
                    j = base + i * unroll + u
                    s_scr[(u + 1) % 2] = scores(jnp.minimum(j + 1, last))
                    st = update(s_scr[u % 2], values_t(j), st)
                return st
            return body

        state = lax.fori_loop(0, (hi - lo) // 4, make_body(lo, 4), state)
        if suffix:
            state = lax.fori_loop(0, blk // 2, make_body(n_pre, 2), state)

            def odd_body(i, st):
                s_scr[1] = scores(last)
                return update(s_scr[0], values_t(last - 1), st)

            state = lax.fori_loop(0, blk % 2, odd_body, state)
            s = s_scr[blk % 2]
            kid = lax.broadcasted_iota(jnp.int32, s.shape, 0)
            qid = lax.broadcasted_iota(jnp.int32, s.shape, 1)
            state = update(jnp.where(kid <= qid, s, -jnp.inf), values_t(last), state)
        m, l, acc = state
        if store:
            st_scr[h, :head_dim] = acc
            st_scr[h, head_dim:head_dim + 8] = l
            st_scr[h, head_dim + 8:] = jnp.broadcast_to(m, (8, rows))
        else:
            o_scr[h] = (acc / jnp.sum(l, axis=0, keepdims=True)).T.astype(o_scr.dtype)

    def o_dst(h):
        return o_full.at[:, pl.ds(pl.multiple_of(my_tp * heads * head_dim + h * head_dim, head_dim), head_dim)]

    def o_copies(h):
        return [pltpu.make_async_remote_copy(src_ref=o_scr.at[h], dst_ref=o_dst(h), send_sem=o_send.at[k, h], recv_sem=o_recv.at[k, h], device_id=dev, device_id_type=MESH) for k, dev in enumerate(peers)]

    def o_own(h):
        return pltpu.make_async_copy(o_scr.at[h], o_dst(h), o_local.at[h])

    def loop_heads(lo_h, hi_h, lo, hi, suffix, load):
        def body(h, carry):
            head_pass(h, lo, hi, suffix, load, not suffix)
            if suffix:
                o_own(h).start()
                for copy in o_copies(h):
                    copy.start()
            return carry
        lax.fori_loop(lo_h, hi_h, body, 0)

    if ring:
        start(0, (0, 1, 2, 3))
        start(1, (0, 1, 2, 3))
        arrived(0, (0, 1))
        loop_heads(0, heads, 0, 4, False, False)
        arrived(0, (2, 3))
        start(0, (4, 5, 6))
        loop_heads(0, heads, 4, 8, False, True)
        arrived(0, (4, 5))
        loop_heads(0, heads, 8, 12, False, True)
        arrived(0, (6,))
        start(0, (7,))
        arrived(1, (0, 1, 2, 3))
        start(1, (4, 5, 6))
        arrived(0, (7,))
        arrived(1, (4, 5, 6))
        start(1, (7,))
        arrived(1, (7,))
        for g in gs:
            for s in range(2 * groups):
                pltpu.make_async_copy(kv_scr.at[g, s], kv_out.at[g, s], kv_save.at[g, s]).start()
        loop_heads(0, heads, 12, 16, True, True)
        for g in gs:
            for s in range(2 * groups):
                pltpu.make_async_copy(kv_scr.at[g, s], kv_out.at[g, s], kv_save.at[g, s]).wait()
            for part in range(2):
                for slot in range(1, groups):
                    kv_copy(part, g, slot).wait_send()
    else:
        def load_copy(g, s):
            return pltpu.make_async_copy(kv_in.at[g, s], kv_scr.at[g, s], kv_recv.at[g, s])
        for g in gs:
            for s in range(2 * groups):
                load_copy(g, s).start()
        for g in gs:
            for s in range(2 * groups):
                load_copy(g, s).wait()
            loop_heads(g * ratio, (g + 1) * ratio, 0, 16, True, False)

    def drain(h, carry):
        o_own(h).wait()
        for copy in o_copies(h):
            copy.wait()
        return carry

    lax.fori_loop(0, heads, drain, 0)


def attention(q, kv, cfg):
    groups, tp, kv_heads, ratio, head_dim, key_rows, rows, ring, upper = (
        cfg[k] for k in ('groups', 'tp', 'kv_heads', 'ratio', 'head_dim', 'key_rows', 'rows', 'ring', 'upper'))
    heads = kv_heads * ratio
    any_spec = pl.BlockSpec(memory_space=pl.ANY)
    row_blk = 1 if upper else 0
    q_spec = pl.BlockSpec((rows, heads * head_dim), lambda i: (row_blk, 0))
    o_shape = jax.ShapeDtypeStruct((rows, tp * heads * head_dim), jnp.bfloat16)
    kv_shape = (kv_heads, 2 * groups, 2 * key_rows, head_dim)
    scratch = [pltpu.VMEM(kv_shape, jnp.bfloat16), pltpu.VMEM((2, key_rows // 2, rows), jnp.float32), pltpu.VMEM((heads, rows, head_dim), jnp.bfloat16)]
    dma = pltpu.SemaphoreType.DMA
    kv_sem, o_sem = dma((kv_heads, 2 * groups)), dma((tp - 1, heads))
    if ring:
        out_shape, out_specs = (o_shape, jax.ShapeDtypeStruct(kv_shape, jnp.bfloat16)), (any_spec, any_spec)
        scratch += [pltpu.VMEM((heads, head_dim + 16, rows), jnp.float32), kv_sem, kv_sem, kv_sem, o_sem, o_sem, dma((heads,))]
    else:
        out_shape, out_specs = o_shape, any_spec
        scratch += [kv_sem, o_sem, o_sem, dma((heads,))]
    n_keys = (2 * groups + (groups + groups // 2 if upper else groups // 2)) * (key_rows // 2)
    return pl.pallas_call(
        functools.partial(attn_kernel, cfg),
        grid=(1,),
        in_specs=[q_spec] + [any_spec] * len(kv),
        out_specs=out_specs,
        out_shape=out_shape,
        scratch_shapes=scratch,
        compiler_params=pltpu.CompilerParams(vmem_limit_bytes=60 * 2**20, dimension_semantics=("arbitrary",), collective_id=1 if upper else 0, has_side_effects=True),
        cost_estimate=pl.CostEstimate(flops=rows * heads * n_keys * 4 * head_dim, bytes_accessed=16 * 2**20, transcendentals=rows * heads * n_keys),
        name="attn_upper" if upper else "attn_lower",
    )(q, *kv)


CHUNK = 256
TILE = 512
N_BUF = 3


def mlp_kernel(cfg, *refs):
    tp, n_o = cfg['tp'], cfg['n_o']
    x_ref = refs[0]
    o_refs = refs[1:1 + n_o]
    (wo_ref, gain_ref, wg_ref, wu_ref, wd_ref, out_ref, wbuf, o_buf, x_buf, y_scr, h_scr, act_scr, part, y_mine, far_buf, near_buf, mine,
     w_sem, in_sem, far_send, far_recv, near_send, near_recv, ag_send, ag_recv, fwd_send, fwd_recv, own_sem) = refs[1 + n_o:]
    rows, width = x_ref.shape
    ff = wg_ref.shape[1]
    n_chunks = rows // CHUNK
    shard = CHUNK // tp
    half = shard // 2
    n_wo, n_gu, n_dn = width // TILE, ff // (TILE // 2), width // TILE
    per = n_wo + n_gu + n_dn
    total = per * n_chunks
    my_tp = lax.axis_index('tp')
    MESH = pl.DeviceIdType.MESH
    above, below = {'tp': (my_tp + 1) % tp}, {'tp': (my_tp + tp - 1) % tp}

    barrier = pltpu.get_barrier_semaphore()
    for dev in (above, below):
        pl.semaphore_signal(barrier, inc=1, device_id=dev, device_id_type=MESH)
    pl.semaphore_wait(barrier, 2)

    def cols(i, n):
        return pl.ds(pl.multiple_of(i * n, n), n)

    def tile_copies(kind, i, slot):
        if kind == 0:
            return [pltpu.make_async_copy(wo_ref.at[:, cols(i, TILE)], wbuf.at[slot], w_sem.at[slot, 0])]
        if kind == 1:
            h = TILE // 2
            return [pltpu.make_async_copy(wg_ref.at[:, cols(i, h)], wbuf.at[slot, :, pl.ds(0, h)], w_sem.at[slot, 0]),
                    pltpu.make_async_copy(wu_ref.at[:, cols(i, h)], wbuf.at[slot, :, pl.ds(h, h)], w_sem.at[slot, 1])]
        return [pltpu.make_async_copy(wd_ref.at[:, cols(i, TILE)], wbuf.at[slot, pl.ds(0, ff)], w_sem.at[slot, 0])]

    def fetch(g):
        t = g % per
        slot = g % N_BUF
        for kind, lo, hi in ((0, 0, n_wo), (1, n_wo, n_wo + n_gu), (2, n_wo + n_gu, per)):
            @pl.when((g < total) & (t >= lo) & (t < hi))
            def _():
                for copy in tile_copies(kind, t - lo, slot):
                    copy.start()

    def tile_loop(c, kind, lo, n, use):
        def body(i, carry):
            g = c * per + lo + i
            slot = g % N_BUF
            for copy in tile_copies(kind, i, slot):
                copy.wait()
            fetch(g + N_BUF - 1)
            use(i, slot)
            return carry
        lax.fori_loop(0, n, body, 0)

    def chunk_rows(c):
        return pl.ds(pl.multiple_of(c * CHUNK, CHUNK), CHUNK)

    def input_copies(c, which):
        o_rows = rows // n_o // CHUNK
        return [pltpu.make_async_copy(x_ref.at[chunk_rows(c)], x_buf, in_sem.at[0]),
                pltpu.make_async_copy(o_refs[which].at[chunk_rows(c - which * o_rows)], o_buf, in_sem.at[1])]

    def fetch_inputs(c):
        o_rows = rows // n_o // CHUNK
        for which in range(n_o):
            @pl.when((c < n_chunks) & (c >= which * o_rows) & (c < (which + 1) * o_rows))
            def _():
                for copy in input_copies(c, which):
                    copy.start()

    def owner_rows(k, lo, n):
        return pl.ds(pl.multiple_of(((my_tp + k) % tp) * shard + lo, n), n)

    def remote(src, dst, send, recv, dev):
        return pltpu.make_async_remote_copy(src_ref=src, dst_ref=dst, send_sem=send, recv_sem=recv, device_id=dev, device_id_type=MESH)

    def far_copies(c):
        p = c % 2
        return [remote(part.at[p, owner_rows(2, 0, half)], far_buf.at[c, 0], far_send.at[c, 0], far_recv.at[c, 0], above),
                remote(part.at[p, owner_rows(2, half, half)], far_buf.at[c, 1], far_send.at[c, 1], far_recv.at[c, 1], below)]

    def near_copies(c):
        p = c % 2
        return [remote(part.at[p, owner_rows(1, 0, shard)], near_buf.at[c, 0], near_send.at[c, 0], near_recv.at[c, 0], above),
                remote(part.at[p, owner_rows(tp - 1, 0, shard)], near_buf.at[c, 1], near_send.at[c, 1], near_recv.at[c, 1], below)]

    def out_rows(c, k, lo, n):
        return out_ref.at[pl.ds(pl.multiple_of(c * CHUNK + ((my_tp + k) % tp) * shard + lo, n), n)]

    def gather_copies(c):
        dst = out_rows(c, 0, 0, shard)
        return [remote(mine.at[c], dst, ag_send.at[c, 0], ag_recv.at[c, 0], above),
                remote(mine.at[c], dst, ag_send.at[c, 1], ag_recv.at[c, 1], below)]

    def forward_copies(c):
        lower, upper = out_rows(c, tp - 1, 0, half), out_rows(c, 1, half, half)
        return [remote(lower, lower, fwd_send.at[c, 0], fwd_recv.at[c, 0], above),
                remote(upper, upper, fwd_send.at[c, 1], fwd_recv.at[c, 1], below)]

    def own_copy(c):
        return pltpu.make_async_copy(mine.at[c], out_rows(c, 0, 0, shard), own_sem.at[c])

    def send_far(c):
        for copy in far_copies(c):
            copy.start()

    def send_near(c):
        for copy in far_copies(c):
            copy.wait_recv()
        p = c % 2

        def add(i, carry):
            cs = cols(i, TILE)
            part[p, owner_rows(1, 0, half), cs] += far_buf[c, 0, :, cs]
            part[p, owner_rows(tp - 1, half, half), cs] += far_buf[c, 1, :, cs]
            return carry
        lax.fori_loop(0, width // TILE, add, 0)
        for copy in near_copies(c):
            copy.start()

    def send_result(c):
        for copy in near_copies(c):
            copy.wait_recv()
        p = c % 2

        def add(i, carry):
            cs = cols(i, TILE)
            total_rows = part[p, owner_rows(0, 0, shard), cs] + near_buf[c, 0, :, cs] + near_buf[c, 1, :, cs]
            mine[c, :, cs] = (y_mine[p, :, cs] + total_rows).astype(mine.dtype)
            return carry
        lax.fori_loop(0, width // TILE, add, 0)
        own_copy(c).start()
        for copy in gather_copies(c):
            copy.start()
        for copy in far_copies(c) + near_copies(c):
            copy.wait_send()

    def forward_result(c):
        for copy in gather_copies(c):
            copy.wait_recv()
        for copy in forward_copies(c):
            copy.start()

    fetch_inputs(0)
    for g in range(N_BUF - 1):
        fetch(g)

    def chunk_body(c, carry):
        p = c % 2
        for copy in input_copies(0, 0):
            copy.wait()

        def proj(i, slot):
            cs = cols(i, TILE)
            y_scr[:, cs] = x_buf[:, cs].astype(jnp.float32) + jnp.dot(o_buf[...], wbuf[slot], preferred_element_type=jnp.float32)

        tile_loop(c, 0, 0, n_wo, proj)
        fetch_inputs(c + 1)

        def square(i, acc):
            y = y_scr[:, cols(i, TILE)]
            y2 = y * y
            for k in range(TILE // 128):
                acc = acc + y2[:, k * 128:(k + 1) * 128]
            return acc
        acc = lax.fori_loop(0, width // TILE, square, jnp.zeros((CHUNK, 128), jnp.float32))
        inv_rms = lax.rsqrt(jnp.sum(acc, axis=1, keepdims=True) / width + NORM_EPS)

        def norm(i, carry):
            cs = cols(i, TILE)
            h_scr[:, cs] = (y_scr[:, cs] * inv_rms * gain_ref[:, cs].astype(jnp.float32)).astype(h_scr.dtype)
            y_mine[p, :, cs] = y_scr[owner_rows(0, 0, shard), cs]
            return carry
        lax.fori_loop(0, width // TILE, norm, 0)

        @pl.when(c > 0)
        def _():
            send_near(c - 1)

        @pl.when(c > 1)
        def _():
            forward_result(c - 2)

        def gated(i, slot):
            gu = jnp.dot(h_scr[...], wbuf[slot], preferred_element_type=jnp.float32)
            gate, up = gu[:, :TILE // 2], gu[:, TILE // 2:]
            act_scr[:, cols(i, TILE // 2)] = (gate * lax.logistic(gate) * up).astype(act_scr.dtype)

        tile_loop(c, 1, n_wo, n_gu, gated)

        @pl.when(c > 0)
        def _():
            send_result(c - 1)

        def down(i, slot):
            part[p, :, cols(i, TILE)] = jnp.dot(act_scr[...], wbuf[slot, :ff], preferred_element_type=jnp.float32)

        tile_loop(c, 2, n_wo + n_gu, n_dn, down)
        send_far(c)
        return carry

    lax.fori_loop(0, n_chunks, chunk_body, 0)
    send_near(n_chunks - 1)
    forward_result(n_chunks - 2)
    send_result(n_chunks - 1)
    forward_result(n_chunks - 1)

    def drain(c, carry):
        own_copy(c).wait()
        for copy in gather_copies(c):
            copy.wait_send()
        for copy in forward_copies(c):
            copy.wait()
        return carry
    lax.fori_loop(0, n_chunks, drain, 0)


def mlp_block(x, o_parts, w_out, gain, w_gate, w_up, w_down, tp):
    rows, width = x.shape
    ff = w_gate.shape[1]
    n = rows // CHUNK
    shard = CHUNK // tp
    any_spec = pl.BlockSpec(memory_space=pl.ANY)
    bf, f32, dma = jnp.bfloat16, jnp.float32, pltpu.SemaphoreType.DMA
    pair = dma((n, 2))
    scratch = [pltpu.VMEM((N_BUF, width, TILE), bf), pltpu.VMEM((CHUNK, width), bf), pltpu.VMEM((CHUNK, width), bf), pltpu.VMEM((CHUNK, width), f32),
               pltpu.VMEM((CHUNK, width), bf), pltpu.VMEM((CHUNK, ff), bf), pltpu.VMEM((2, CHUNK, width), f32), pltpu.VMEM((2, shard, width), f32),
               pltpu.VMEM((n, 2, shard // 2, width), f32), pltpu.VMEM((n, 2, shard, width), f32), pltpu.VMEM((n, shard, width), bf),
               dma((N_BUF, 2)), dma((2,)), pair, pair, pair, pair, pair, pair, pair, pair, dma((n,))]
    flops = 2 * rows * width * (w_out.shape[0] + 3 * ff)
    return pl.pallas_call(
        functools.partial(mlp_kernel, dict(tp=tp, n_o=len(o_parts))),
        grid=(1,),
        in_specs=[any_spec] * (2 + len(o_parts)) + [pl.BlockSpec((1, width), lambda i: (0, 0))] + [any_spec] * 3,
        out_specs=any_spec,
        out_shape=jax.ShapeDtypeStruct(x.shape, x.dtype),
        scratch_shapes=scratch,
        compiler_params=pltpu.CompilerParams(vmem_limit_bytes=63 * 2**20, dimension_semantics=("arbitrary",), collective_id=2, has_side_effects=True),
        cost_estimate=pl.CostEstimate(flops=flops, bytes_accessed=500 * 2**20, transcendentals=rows * ff),
        name="mlp",
    )(x, *o_parts, w_out, gain.reshape(1, width), w_gate, w_up, w_down)


def solution(mesh):
    groups = mesh.shape['cp']
    tp = mesh.shape['tp']

    def local_layer(x_loc, kp_loc, vp_loc, norm_attn, w_query, w_key, w_value, w_out, norm_mlp, w_gate, w_up, w_down):
        rows_loc = x_loc.shape[0]
        blk_len = rows_loc // 2
        pre_dev, kv_loc, head_dim = kp_loc.shape
        heads_loc = w_query.shape[1] // head_dim
        prefix_len = pre_dev * groups
        my_cp = lax.axis_index('cp')

        def bundle_of(k, v):
            kt = jnp.moveaxis(k, 1, 0)
            vt = v.reshape(rows_loc // head_dim, head_dim, kv_loc, head_dim).transpose(2, 0, 3, 1).reshape(kv_loc, rows_loc, head_dim)
            return jnp.concatenate([kt, vt], axis=1)

        w_rows = w_out.shape[0] // groups
        w_out_full = lax.all_gather(lax.dynamic_slice_in_dim(w_out, my_cp * w_rows, w_rows, 0), ('tp', 'cp'), tiled=True)

        local_row = jnp.arange(rows_loc, dtype=jnp.int32)
        blk_idx = jnp.where(local_row < blk_len, my_cp, 2 * groups - 1 - my_cp)
        q_pos = prefix_len + blk_idx * blk_len + local_row % blk_len
        cos_tab, sin_tab = rope_tables(q_pos, head_dim)
        hidden = rms_norm(x_loc, norm_attn)
        k_proj = jnp.dot(hidden, w_key, preferred_element_type=jnp.float32).reshape(rows_loc, kv_loc, head_dim)
        k_new = apply_rope(k_proj, cos_tab, sin_tab).astype(jnp.bfloat16)
        v_new = jnp.dot(hidden, w_value, preferred_element_type=jnp.float32).astype(jnp.bfloat16).reshape(rows_loc, kv_loc, head_dim)
        q_proj = jnp.dot(hidden, w_query, preferred_element_type=jnp.float32).reshape(rows_loc, heads_loc, head_dim)
        q_rot = apply_rope(q_proj, cos_tab, sin_tab).astype(jnp.bfloat16).reshape(rows_loc, heads_loc * head_dim)

        cfg = dict(groups=groups, tp=tp, kv_heads=kv_loc, ratio=heads_loc // kv_loc, head_dim=head_dim, key_rows=rows_loc, rows=blk_len)
        o_a, kv_all = attention(q_rot, [bundle_of(kp_loc, vp_loc), bundle_of(k_new, v_new)], dict(cfg, ring=True, upper=False))

        o_b = attention(q_rot, [kv_all], dict(cfg, ring=False, upper=True))
        x_out = mlp_block(x_loc, [o_a, o_b], w_out_full, norm_mlp, w_gate, w_up, w_down, tp)
        return x_out, k_new, v_new

    row_spec = P(('dp', 'cp'), None)
    kv_spec = P(('dp', 'cp'), 'tp', None)
    col_spec = P(None, 'tp')
    row_split = P('tp', None)
    vec_spec = P(None)
    return jax.shard_map(local_layer, mesh=mesh, in_specs=(row_spec, kv_spec, kv_spec, vec_spec, col_spec, col_spec, col_spec, row_split, vec_spec, col_spec, col_spec, row_split), out_specs=(row_spec, kv_spec, kv_spec), check_vma=False)
```

time: 1570 us -> 626 us (0.40)
  waiting for transfers between devices: 673 us -> 0.07 us
  matrix products: 584 us -> 23.7 us
  Pallas kernels: 0 us -> 535 us
  other arithmetic: 236 us -> 15.6 us
  local copies, waits for them, and re-layouts: 53.6 us -> 31.1 us
    psum x2 -> x0, waiting for transfers between devices: 576 us -> none  [the longest x1 290 us: local_layer(): lax.psum(jnp.dot(attn_heads, w_out, preferred_element_type=jnp.float32),...]
    dot_general x20 -> x0, matrix products: 560 us -> none  [the longest x8 227 us: attend_step(): jnp.einsum('sgrk,kgd->sgrd', weights.astype(jnp.bfloat16), v_blk, preferr...]
    pallas_call x0 -> x3, Pallas kernels: none -> 535 us  [the longest x2 285 us: attention(): pl.pallas_call(functools.partial(attn_kernel, cfg), grid=(1,), in_specs=[...]
    reduce_sum x8 -> x0, other arithmetic: 173 us -> none  [attend_step(): denom_sum = denom_sum * correction + jnp.sum(weights, axis=-1)]
    ppermute x14 -> x0, waiting for transfers between devices: 97 us -> none  [step_body(): k_cur, v_cur = lax.ppermute((k_cur, v_cur), 'cp', perm_pairs)]
    while x22 -> x0, local copies, waits for them, and re-layouts: 28 us -> none
    convert_element_type x3 -> x1, other arithmetic: 26.7 us -> 0.01 us  [rope_tables(): angles = positions.astype(jnp.float32)[:, None] * inv_freq[None, :]]
  transfers between devices with their start and end apart: 16 -> 1, of which waited for: 9 -> 0; matrix products, arithmetic and copies ran while one was open for 23% -> 9% of each run, Pallas kernels for 0% -> 46%
where the time goes in v2:
time: 626 us; the launch traced here: 620 us
  Pallas kernels  535 us (85%)
  local copies, waits for them, and re-layouts  31.1 us (5%)
  matrix products  23.7 us (4%)
  other arithmetic  15.6 us (2%)
  between operations  14.7 us (2%)
    pallas_call x2, Pallas kernels, attention(): pl.pallas_call(functools.partial(attn_kernel, cfg), grid=(1,), in_specs=[...  285 us
    pallas_call x1, Pallas kernels, mlp_block(): pl.pallas_call(functools.partial(mlp_kernel, dict(tp=tp, n_o=len(o_parts)...  250 us
    unnamed x30, local copies, waits for them, and re-layouts  24 us
    dot_general x1, matrix products, local_layer(): jnp.dot(hidden, w_query, preferred_element_type=jnp.float32)  14 us
  transfers between devices with their start and end apart: 1, of which 0 were waited for; matrix products, arithmetic and copies ran while one was open for 9% of the time, Pallas kernels for 46%

profile of v2, /device:TPU:96, one launch (start us, length us, event | category | flops | bytes accessed | tf_op | source)
XLA Modules:
  0.0 619.7 jit_solution(14730061547371771632)
XLA Ops:
  7.3 2.4 constant_dynamic-slice_fusion
  9.8 0.7 convert_element_type.26
  10.5 5.2 fusion
  15.7 0.5 copy-done
  16.2 3.0 fusion.9
  19.3 0.3 copy.33
  19.6 1.3 copy.34
  20.9 6.7 %convolution_convert_fusion = bf16[1024,256]{0,1:T(8,128)(2,1)S(1)} fusion(bf16[4096,256]{1,0:T(8,128)(2,1)} %param.18, bf16[1024,4096]{1,0:T(8,128)(2,1)} %refs_0_.1, f32[4096]{0:T(1024)S(1)} %convert_element_type.26, f32[1024]{0:T(1024)S(1)} %add_rsqrt_fusion), kind=kOutput, calls=%fused_computation.9 | convolution fusion | flops 2164523008 | bytes 11030528 | tf_op jit(solution)/shard_map/dot_general | solution.py:541
  27.7 0.8 copy-done.2
  28.5 0.1 copy.36
  28.6 0.9 copy.28
  29.5 0.9 copy.40
  30.4 1.2 copy.25
  31.6 14.0 %fusion.11 = f32[1024,1024]{0,1:T(8,128)S(1)} fusion(bf16[4096,1024]{1,0:T(8,128)(2,1)} %param.16, bf16[1024,4096]{1,0:T(8,128)(2,1)} %refs_0_.1, f32[4096]{0:T(1024)S(1)} %convert_element_type.26, f32[1024]{0:T(1024)S(1)} %add_rsqrt_fusion), kind=kOutput, calls=%fused_computation.30 | convolution fusion | flops 8606711808 | bytes 20992000 | tf_op jit(solution)/shard_map/dot_general | solution.py:542
  45.6 1.7 fusion.13
  47.3 3.9 copy.31
  51.3 2.8 copy.32
  54.1 1.9 multiply_cosine_fusion
  56.0 4.2 subtract_convert_fusion
  60.2 1.2 pad_maximum_fusion
  61.4 1.9 copy.39
  63.3 0.6 reshape.114.refs_4_
  63.9 0.3 subtract_convert_fusion.1
  64.3 0.3 pad_maximum_fusion.3
  64.6 1.3 copy.29
  65.9 2.2 copy.30
  68.1 0.3 fusion.18
  68.4 1.5 pad_maximum_fusion.1
  69.9 170.0 %attn_lower.1 = (bf16[512,4096]{1,0:T(8,128)(2,1)}, bf16[2,16,2048,128]{3,2,1,0:T(8,128)(2,1)}) custom-call(bf16[1024,1024]{1,0:T(8,128)(2,1)} %bitcast.29, bf16[2,2048,128]{2,1,0:T(8,128)(2,1)} %get-tuple-element.23.refs_1_, bf16[2,2048,128]{2,1,0:T(8,128)(2,1)} %get-tuple-element.24.refs_2_), custom_call_target="tpu_custom_call" | custom-call | flops 21474836480 | bytes 16777216 | tf_op jit(solution)/shard_map/attn_lower/pallas_call | solution.py:252
  240.0 115.0 %attn_upper.1.refs_2_ = bf16[512,4096]{1,0:T(8,128)(2,1)} custom-call(bf16[1024,1024]{1,0:T(8,128)(2,1)} %bitcast.30, bf16[2,16,2048,128]{3,2,1,0:T(8,128)(2,1)} %get-tuple-element.6.refs_1_), custom_call_target="tpu_custom_call" | custom-call | flops 30064771072 | bytes 16777216 | tf_op jit(solution)/shard_map/attn_upper/pallas_call | solution.py:252
  354.9 249.6 %mlp.1 = bf16[1024,4096]{1,0:T(8,128)(2,1)} custom-call(bf16[1024,4096]{1,0:T(8,128)(2,1)} %refs_0_.1, bf16[512,4096]{1,0:T(8,128)(2,1)} %get-tuple-element.5.refs_1_, bf16[512,4096]{1,0:T(8,128)(2,1)} %attn_upper.1.refs_2_, bf16[4096,4096]{1,0:T(8,128)(2,1)} %all-gather.2.cloned.1.call-done.refs_3_, bf16[1,4096]{1,0:T(2,128)(2,1)} %reshape.114.refs_4_, ...), custom_call_target="tpu_custom_call" | custom-call | flops 124554051584 | bytes 524288000 | tf_op jit(solution)/shard_map/mlp/pallas_call | solution.py:501
  604.6 7.9 %copy.42 = bf16[1024,4096]{1,0:T(8,128)(2,1)} copy(bf16[1024,4096]{1,0:T(8,128)(2,1)} %mlp.1) | data formatting | bytes 16777216
  (25 shorter events, 0.3 us)
Async XLA Ops:
  7.2 347.8 %all-gather.2.cloned.1.call-start = ((), (), s32[]{:S(2)}) async-start(), calls=%async_computation | async-start | bytes 34603008 | tf_op jit(solution)/shard_map/all_gather | solution.py:532
  7.3 8.5 %copy-start.9 = (bf16[4096,256]{1,0:T(8,128)(2,1)S(1)}, bf16[4096,256]{1,0:T(8,128)(2,1)}, u32[]{:S(2)}) copy-start(bf16[4096,256]{1,0:T(8,128)(2,1)} %param.17) | copy-start | bytes 6291460
  10.5 5.8 copy-start
  20.9 8.6 %copy-start.6 = (bf16[1024,2,128]{2,1,0:T(2,128)(2,1)S(1)}, bf16[1024,2,128]{2,1,0:T(2,128)(2,1)}, u32[]{:S(2)}) copy-start(bf16[1024,2,128]{2,1,0:T(2,128)(2,1)} %param.13) | copy-start | bytes 1572868
  20.9 9.4 %copy-start.7 = (bf16[1024,2,128]{2,1,0:T(2,128)(2,1)S(1)}, bf16[1024,2,128]{2,1,0:T(2,128)(2,1)}, u32[]{:S(2)}) copy-start(bf16[1024,2,128]{2,1,0:T(2,128)(2,1)} %param.14) | copy-start | bytes 1572868
  27.7 0.8 copy-start.2
  60.2 3.1 copy-start.8
  60.2 3.7 copy-start.1
  64.3 4.2 copy-start.3
  64.3 4.2 copy-start.4
  64.3 4.2 copy-start.5
Sparse Core Ops, SparseCore 0:
  10.1 149.1 all-gather.1

commit v3 on v2

--- a/solution.py
+++ b/solution.py
@@ -35,13 +35,10 @@
 
 
 def attn_kernel(cfg, *refs):
-    groups, tp, kv_heads, ratio, head_dim, key_rows, rows, ring, upper = (
-        cfg[k] for k in ('groups', 'tp', 'kv_heads', 'ratio', 'head_dim', 'key_rows', 'rows', 'ring', 'upper'))
+    groups, tp, kv_heads, ratio, head_dim, key_rows, rows = (cfg[k] for k in ('groups', 'tp', 'kv_heads', 'ratio', 'head_dim', 'key_rows', 'rows'))
     heads = kv_heads * ratio
-    if ring:
-        q_ref, pre_ref, suf_ref, o_full, kv_out, kv_scr, s_scr, o_scr, st_scr, kv_send, kv_recv, kv_save, o_send, o_recv, o_local = refs
-    else:
-        q_ref, kv_in, o_full, kv_scr, s_scr, o_scr, kv_recv, o_send, o_recv, o_local = refs
+    (q_raw, cos_ref, sin_ref, pre_ref, suf_ref, w_ref, o_full, w_full, q_ref, kv_scr, s_scr, o_scr, st_scr, kv_send, kv_recv, o_send, o_recv, o_local,
+     wn_send, wn_recv, wf_send, wf_recv, wx_send, wx_recv, ws_send, ws_recv) = refs
     me, my_tp = lax.axis_index('cp'), lax.axis_index('tp')
     my_x, my_core = me // 2, me % 2
     half = key_rows // 2
@@ -53,14 +50,14 @@
     peers = [{'tp': (my_tp + k) % tp} for k in range(1, tp)]
 
     barrier = pltpu.get_barrier_semaphore()
-    greet = peers + ([sib, x_next, x_prev] if ring else [])
+    greet = peers + [sib, x_next, x_prev]
     for dev in greet:
         pl.semaphore_signal(barrier, inc=1, device_id=dev, device_id_type=MESH)
     pl.semaphore_wait(barrier, len(greet))
 
     def kv_copy(part, g, slot):
         base = part * groups
-        src_own = (pre_ref, suf_ref)[part].at[g] if ring else None
+        src_own = (pre_ref, suf_ref)[part].at[g]
         dst = kv_scr.at[g, base + slot]
         if slot == 0:
             return pltpu.make_async_copy(src_own, dst, kv_recv.at[g, base])
@@ -88,8 +85,48 @@
                 copy = kv_copy(part, g, slot)
                 copy.wait() if slot == 0 else copy.wait_recv()
 
-    blk = (2 * groups - 1 - me) if upper else me
     n_pre = 2 * groups
+
+    quarter = w_ref.shape[0] // 4
+    w_half = quarter // 2
+    my_quarter = 2 * (my_x % 2) + my_core
+    x_quarter = 2 * (1 - my_x % 2) + my_core
+    above, below = {'tp': (my_tp + 1) % tp}, {'tp': (my_tp + tp - 1) % tp}
+    ks = (tp - 1, 1, 2)
+
+    def w_rows(k, which, lo, n):
+        return w_full.at[pl.ds(pl.multiple_of(((my_tp + k) % tp) * w_ref.shape[0] + which * quarter + lo, n), n)]
+
+    def remote(src, dst, send, recv, dev):
+        return pltpu.make_async_remote_copy(src_ref=src, dst_ref=dst, send_sem=send, recv_sem=recv, device_id=dev, device_id_type=MESH)
+
+    def w_near():
+        src = w_ref.at[pl.ds(pl.multiple_of(my_quarter * quarter, quarter), quarter)]
+        return [remote(src, w_rows(0, my_quarter, 0, quarter), wn_send.at[i], wn_recv.at[i], dev) for i, dev in enumerate((above, below))]
+
+    def w_far():
+        out = []
+        for i, (k, dev) in enumerate(((tp - 1, above), (1, below))):
+            piece = w_rows(k, my_quarter, i * w_half, w_half)
+            out.append(remote(piece, piece, wf_send.at[i], wf_recv.at[i], dev))
+        return out
+
+    def w_x(n):
+        out = []
+        for i, dev in enumerate((x_next, x_prev)):
+            piece = w_rows(ks[n], my_quarter, i * w_half, w_half)
+            out.append(remote(piece, piece, wx_send.at[i, n], wx_recv.at[i, n], dev))
+        return out
+
+    def w_sib(n, second):
+        piece = w_rows(ks[n], x_quarter if second else my_quarter, 0, quarter)
+        return remote(piece, piece, ws_send.at[int(second), n], ws_recv.at[int(second), n], sib)
+
+    def rope(h, carry):
+        cs = pl.ds(pl.multiple_of(h * head_dim, head_dim), head_dim)
+        x = q_raw[:, cs]
+        q_ref[:, cs] = (x * cos_ref[...] + pltpu.roll(x, head_dim // 2, 1) * sin_ref[...]).astype(q_ref.dtype)
+        return carry
 
     def locate(j):
         b = j - n_pre
@@ -101,9 +138,10 @@
         pre = j < n_pre
         return jnp.where(pre, j // 2, groups + s_slot), jnp.where(pre, (j % 2) * half, jnp.where(lower, 0, half))
 
-    def head_pass(h, lo, hi, suffix, load, store):
+    def head_pass(upper, h, lo, hi, suffix, load, store):
         g = h // ratio
-        q = q_ref[:, pl.ds(pl.multiple_of(h * head_dim, head_dim), head_dim)]
+        blk = (2 * groups - 1 - me) if upper else me
+        q = q_ref[upper * rows:(upper + 1) * rows, pl.ds(pl.multiple_of(h * head_dim, head_dim), head_dim)]
 
         def scores(j):
             slot, off = locate(j)
@@ -161,105 +199,113 @@
             st_scr[h, head_dim:head_dim + 8] = l
             st_scr[h, head_dim + 8:] = jnp.broadcast_to(m, (8, rows))
         else:
-            o_scr[h] = (acc / jnp.sum(l, axis=0, keepdims=True)).T.astype(o_scr.dtype)
-
-    def o_dst(h):
-        return o_full.at[:, pl.ds(pl.multiple_of(my_tp * heads * head_dim + h * head_dim, head_dim), head_dim)]
-
-    def o_copies(h):
-        return [pltpu.make_async_remote_copy(src_ref=o_scr.at[h], dst_ref=o_dst(h), send_sem=o_send.at[k, h], recv_sem=o_recv.at[k, h], device_id=dev, device_id_type=MESH) for k, dev in enumerate(peers)]
-
-    def o_own(h):
-        return pltpu.make_async_copy(o_scr.at[h], o_dst(h), o_local.at[h])
-
-    def loop_heads(lo_h, hi_h, lo, hi, suffix, load):
+            o_scr[upper * heads + h] = (acc / jnp.sum(l, axis=0, keepdims=True)).T.astype(o_scr.dtype)
+
+    def o_dst(upper, h):
+        return o_full.at[upper * rows:(upper + 1) * rows, pl.ds(pl.multiple_of(my_tp * heads * head_dim + h * head_dim, head_dim), head_dim)]
+
+    def o_copies(upper, h):
+        i = upper * heads + h
+        return [remote(o_scr.at[i], o_dst(upper, h), o_send.at[k, i], o_recv.at[k, i], dev) for k, dev in enumerate(peers)]
+
+    def o_own(upper, h):
+        return pltpu.make_async_copy(o_scr.at[upper * heads + h], o_dst(upper, h), o_local.at[upper * heads + h])
+
+    def loop_heads(upper, lo_h, hi_h, lo, hi, suffix, load):
         def body(h, carry):
-            head_pass(h, lo, hi, suffix, load, not suffix)
+            head_pass(upper, h, lo, hi, suffix, load, not suffix)
             if suffix:
-                o_own(h).start()
-                for copy in o_copies(h):
+                o_own(upper, h).start()
+                for copy in o_copies(upper, h):
                     copy.start()
             return carry
         lax.fori_loop(lo_h, hi_h, body, 0)
 
-    if ring:
-        start(0, (0, 1, 2, 3))
-        start(1, (0, 1, 2, 3))
-        arrived(0, (0, 1))
-        loop_heads(0, heads, 0, 4, False, False)
-        arrived(0, (2, 3))
-        start(0, (4, 5, 6))
-        loop_heads(0, heads, 4, 8, False, True)
-        arrived(0, (4, 5))
-        loop_heads(0, heads, 8, 12, False, True)
-        arrived(0, (6,))
-        start(0, (7,))
-        arrived(1, (0, 1, 2, 3))
-        start(1, (4, 5, 6))
-        arrived(0, (7,))
-        arrived(1, (4, 5, 6))
-        start(1, (7,))
-        arrived(1, (7,))
-        for g in gs:
-            for s in range(2 * groups):
-                pltpu.make_async_copy(kv_scr.at[g, s], kv_out.at[g, s], kv_save.at[g, s]).start()
-        loop_heads(0, heads, 12, 16, True, True)
-        for g in gs:
-            for s in range(2 * groups):
-                pltpu.make_async_copy(kv_scr.at[g, s], kv_out.at[g, s], kv_save.at[g, s]).wait()
-            for part in range(2):
-                for slot in range(1, groups):
-                    kv_copy(part, g, slot).wait_send()
-    else:
-        def load_copy(g, s):
-            return pltpu.make_async_copy(kv_in.at[g, s], kv_scr.at[g, s], kv_recv.at[g, s])
-        for g in gs:
-            for s in range(2 * groups):
-                load_copy(g, s).start()
-        for g in gs:
-            for s in range(2 * groups):
-                load_copy(g, s).wait()
-            loop_heads(g * ratio, (g + 1) * ratio, 0, 16, True, False)
-
-    def drain(h, carry):
-        o_own(h).wait()
-        for copy in o_copies(h):
-            copy.wait()
-        return carry
-
-    lax.fori_loop(0, heads, drain, 0)
-
-
-def attention(q, kv, cfg):
-    groups, tp, kv_heads, ratio, head_dim, key_rows, rows, ring, upper = (
-        cfg[k] for k in ('groups', 'tp', 'kv_heads', 'ratio', 'head_dim', 'key_rows', 'rows', 'ring', 'upper'))
+    start(0, (0, 1, 2, 3))
+    for copy in w_near():
+        copy.start()
+    start(1, (0, 1, 2, 3))
+    lax.fori_loop(0, heads, rope, 0)
+    arrived(0, (0, 1))
+    loop_heads(0, 0, heads, 0, 4, False, False)
+    arrived(0, (2, 3))
+    start(0, (4, 5, 6))
+    loop_heads(0, 0, heads, 4, 8, False, True)
+    arrived(0, (4, 5))
+    loop_heads(0, 0, heads, 8, 12, False, True)
+    arrived(0, (6,))
+    start(0, (7,))
+    arrived(1, (0, 1, 2, 3))
+    start(1, (4, 5, 6))
+    for copy in w_near():
+        copy.wait_recv()
+    for copy in w_far():
+        copy.start()
+    arrived(0, (7,))
+    arrived(1, (4, 5, 6))
+    start(1, (7,))
+    for n in range(2):
+        w_sib(n, False).start()
+        for copy in w_x(n):
+            copy.start()
+    arrived(1, (7,))
+    loop_heads(0, 0, heads, 12, 16, True, True)
+    for copy in w_far():
+        copy.wait_recv()
+    w_sib(2, False).start()
+    for copy in w_x(2):
+        copy.start()
+    loop_heads(1, 0, heads // 2, 0, 16, True, False)
+    for n in range(3):
+        for copy in w_x(n):
+            copy.wait_recv()
+        w_sib(n, True).start()
+    loop_heads(1, heads // 2, heads, 0, 16, True, False)
+
+    for g in gs:
+        for part in range(2):
+            for slot in range(1, groups):
+                kv_copy(part, g, slot).wait_send()
+    for copy in w_near() + w_far():
+        copy.wait_send()
+    for n in range(3):
+        for copy in w_x(n):
+            copy.wait_send()
+        for second in (False, True):
+            w_sib(n, second).wait()
+
+    for upper in range(2):
+        def drain(h, carry):
+            o_own(upper, h).wait()
+            for copy in o_copies(upper, h):
+                copy.wait()
+            return carry
+        lax.fori_loop(0, heads, drain, 0)
+
+
+def attention(q, cos, sin, pre, suf, w_out, cfg):
+    groups, tp, kv_heads, ratio, head_dim, key_rows, rows = (cfg[k] for k in ('groups', 'tp', 'kv_heads', 'ratio', 'head_dim', 'key_rows', 'rows'))
     heads = kv_heads * ratio
+    bf, f32, dma = jnp.bfloat16, jnp.float32, pltpu.SemaphoreType.DMA
     any_spec = pl.BlockSpec(memory_space=pl.ANY)
-    row_blk = 1 if upper else 0
-    q_spec = pl.BlockSpec((rows, heads * head_dim), lambda i: (row_blk, 0))
-    o_shape = jax.ShapeDtypeStruct((rows, tp * heads * head_dim), jnp.bfloat16)
+    whole = lambda arr: pl.BlockSpec(arr.shape, lambda i: (0, 0))
     kv_shape = (kv_heads, 2 * groups, 2 * key_rows, head_dim)
-    scratch = [pltpu.VMEM(kv_shape, jnp.bfloat16), pltpu.VMEM((2, key_rows // 2, rows), jnp.float32), pltpu.VMEM((heads, rows, head_dim), jnp.bfloat16)]
-    dma = pltpu.SemaphoreType.DMA
-    kv_sem, o_sem = dma((kv_heads, 2 * groups)), dma((tp - 1, heads))
-    if ring:
-        out_shape, out_specs = (o_shape, jax.ShapeDtypeStruct(kv_shape, jnp.bfloat16)), (any_spec, any_spec)
-        scratch += [pltpu.VMEM((heads, head_dim + 16, rows), jnp.float32), kv_sem, kv_sem, kv_sem, o_sem, o_sem, dma((heads,))]
-    else:
-        out_shape, out_specs = o_shape, any_spec
-        scratch += [kv_sem, o_sem, o_sem, dma((heads,))]
-    n_keys = (2 * groups + (groups + groups // 2 if upper else groups // 2)) * (key_rows // 2)
+    kv_sem, o_sem = dma((kv_heads, 2 * groups)), dma((tp - 1, 2 * heads))
+    scratch = [pltpu.VMEM(q.shape, bf), pltpu.VMEM(kv_shape, bf), pltpu.VMEM((2, key_rows // 2, rows), f32), pltpu.VMEM((2 * heads, rows, head_dim), bf),
+               pltpu.VMEM((heads, head_dim + 16, rows), f32), kv_sem, kv_sem, o_sem, o_sem, dma((2 * heads,)),
+               dma((2,)), dma((2,)), dma((2,)), dma((2,)), dma((2, 3)), dma((2, 3)), dma((2, 3)), dma((2, 3))]
+    n_keys = (4 * groups + 2 * groups) * (key_rows // 2)
     return pl.pallas_call(
         functools.partial(attn_kernel, cfg),
         grid=(1,),
-        in_specs=[q_spec] + [any_spec] * len(kv),
-        out_specs=out_specs,
-        out_shape=out_shape,
+        in_specs=[whole(q), whole(cos), whole(sin)] + [any_spec] * 3,
+        out_specs=(any_spec, any_spec),
+        out_shape=(jax.ShapeDtypeStruct((2 * rows, tp * heads * head_dim), bf), jax.ShapeDtypeStruct((tp * w_out.shape[0], w_out.shape[1]), bf)),
         scratch_shapes=scratch,
-        compiler_params=pltpu.CompilerParams(vmem_limit_bytes=60 * 2**20, dimension_semantics=("arbitrary",), collective_id=1 if upper else 0, has_side_effects=True),
+        compiler_params=pltpu.CompilerParams(vmem_limit_bytes=60 * 2**20, dimension_semantics=("arbitrary",), collective_id=0, has_side_effects=True),
         cost_estimate=pl.CostEstimate(flops=rows * heads * n_keys * 4 * head_dim, bytes_accessed=16 * 2**20, transcendentals=rows * heads * n_keys),
-        name="attn_upper" if upper else "attn_lower",
-    )(q, *kv)
+        name="attn",
+    )(q, cos, sin, pre, suf, w_out)
 
 
 CHUNK = 256
@@ -271,7 +317,7 @@
     tp, n_o = cfg['tp'], cfg['n_o']
     x_ref = refs[0]
     o_refs = refs[1:1 + n_o]
-    (wo_ref, gain_ref, wg_ref, wu_ref, wd_ref, out_ref, wbuf, o_buf, x_buf, y_scr, h_scr, act_scr, part, y_mine, far_buf, near_buf, mine,
+    (wo_ref, wown_ref, gain_ref, wg_ref, wu_ref, wd_ref, out_ref, wbuf, o_buf, x_buf, y_scr, h_scr, act_scr, part, y_mine, far_buf, near_buf, mine,
      w_sem, in_sem, far_send, far_recv, near_send, near_recv, ag_send, ag_recv, fwd_send, fwd_recv, own_sem) = refs[1 + n_o:]
     rows, width = x_ref.shape
     ff = wg_ref.shape[1]
@@ -295,7 +341,13 @@
 
     def tile_copies(kind, i, slot):
         if kind == 0:
-            return [pltpu.make_async_copy(wo_ref.at[:, cols(i, TILE)], wbuf.at[slot], w_sem.at[slot, 0])]
+            n = wown_ref.shape[0]
+            out = []
+            for k in range(tp):
+                part_rows = pl.ds(pl.multiple_of(((my_tp + k) % tp) * n, n), n)
+                src = wo_ref.at[part_rows, cols(i, TILE)] if k else wown_ref.at[:, cols(i, TILE)]
+                out.append(pltpu.make_async_copy(src, wbuf.at[slot, part_rows], w_sem.at[slot, k]))
+            return out
         if kind == 1:
             h = TILE // 2
             return [pltpu.make_async_copy(wg_ref.at[:, cols(i, h)], wbuf.at[slot, :, pl.ds(0, h)], w_sem.at[slot, 0]),
@@ -485,7 +537,7 @@
     lax.fori_loop(0, n_chunks, drain, 0)
 
 
-def mlp_block(x, o_parts, w_out, gain, w_gate, w_up, w_down, tp):
+def mlp_block(x, o_parts, w_out, w_own, gain, w_gate, w_up, w_down, tp):
     rows, width = x.shape
     ff = w_gate.shape[1]
     n = rows // CHUNK
@@ -496,19 +548,19 @@
     scratch = [pltpu.VMEM((N_BUF, width, TILE), bf), pltpu.VMEM((CHUNK, width), bf), pltpu.VMEM((CHUNK, width), bf), pltpu.VMEM((CHUNK, width), f32),
                pltpu.VMEM((CHUNK, width), bf), pltpu.VMEM((CHUNK, ff), bf), pltpu.VMEM((2, CHUNK, width), f32), pltpu.VMEM((2, shard, width), f32),
                pltpu.VMEM((n, 2, shard // 2, width), f32), pltpu.VMEM((n, 2, shard, width), f32), pltpu.VMEM((n, shard, width), bf),
-               dma((N_BUF, 2)), dma((2,)), pair, pair, pair, pair, pair, pair, pair, pair, dma((n,))]
+               dma((N_BUF, tp)), dma((2,)), pair, pair, pair, pair, pair, pair, pair, pair, dma((n,))]
     flops = 2 * rows * width * (w_out.shape[0] + 3 * ff)
     return pl.pallas_call(
         functools.partial(mlp_kernel, dict(tp=tp, n_o=len(o_parts))),
         grid=(1,),
-        in_specs=[any_spec] * (2 + len(o_parts)) + [pl.BlockSpec((1, width), lambda i: (0, 0))] + [any_spec] * 3,
+        in_specs=[any_spec] * (3 + len(o_parts)) + [pl.BlockSpec((1, width), lambda i: (0, 0))] + [any_spec] * 3,
         out_specs=any_spec,
         out_shape=jax.ShapeDtypeStruct(x.shape, x.dtype),
         scratch_shapes=scratch,
         compiler_params=pltpu.CompilerParams(vmem_limit_bytes=63 * 2**20, dimension_semantics=("arbitrary",), collective_id=2, has_side_effects=True),
         cost_estimate=pl.CostEstimate(flops=flops, bytes_accessed=500 * 2**20, transcendentals=rows * ff),
         name="mlp",
-    )(x, *o_parts, w_out, gain.reshape(1, width), w_gate, w_up, w_down)
+    )(x, *o_parts, w_out, w_own, gain.reshape(1, width), w_gate, w_up, w_down)
 
 
 def solution(mesh):
@@ -527,9 +579,6 @@
             kt = jnp.moveaxis(k, 1, 0)
             vt = v.reshape(rows_loc // head_dim, head_dim, kv_loc, head_dim).transpose(2, 0, 3, 1).reshape(kv_loc, rows_loc, head_dim)
             return jnp.concatenate([kt, vt], axis=1)
-
-        w_rows = w_out.shape[0] // groups
-        w_out_full = lax.all_gather(lax.dynamic_slice_in_dim(w_out, my_cp * w_rows, w_rows, 0), ('tp', 'cp'), tiled=True)
 
         local_row = jnp.arange(rows_loc, dtype=jnp.int32)
         blk_idx = jnp.where(local_row < blk_len, my_cp, 2 * groups - 1 - my_cp)
@@ -539,14 +588,13 @@
         k_proj = jnp.dot(hidden, w_key, preferred_element_type=jnp.float32).reshape(rows_loc, kv_loc, head_dim)
         k_new = apply_rope(k_proj, cos_tab, sin_tab).astype(jnp.bfloat16)
         v_new = jnp.dot(hidden, w_value, preferred_element_type=jnp.float32).astype(jnp.bfloat16).reshape(rows_loc, kv_loc, head_dim)
-        q_proj = jnp.dot(hidden, w_query, preferred_element_type=jnp.float32).reshape(rows_loc, heads_loc, head_dim)
-        q_rot = apply_rope(q_proj, cos_tab, sin_tab).astype(jnp.bfloat16).reshape(rows_loc, heads_loc * head_dim)
+        q_proj = jnp.dot(hidden, w_query, preferred_element_type=jnp.float32)
+        cos_all = jnp.concatenate([cos_tab, cos_tab], axis=1)
+        sin_all = jnp.concatenate([-sin_tab, sin_tab], axis=1)
 
         cfg = dict(groups=groups, tp=tp, kv_heads=kv_loc, ratio=heads_loc // kv_loc, head_dim=head_dim, key_rows=rows_loc, rows=blk_len)
-        o_a, kv_all = attention(q_rot, [bundle_of(kp_loc, vp_loc), bundle_of(k_new, v_new)], dict(cfg, ring=True, upper=False))
-
-        o_b = attention(q_rot, [kv_all], dict(cfg, ring=False, upper=True))
-        x_out = mlp_block(x_loc, [o_a, o_b], w_out_full, norm_mlp, w_gate, w_up, w_down, tp)
+        o_full, w_full = attention(q_proj, cos_all, sin_all, bundle_of(kp_loc, vp_loc), bundle_of(k_new, v_new), w_out, cfg)
+        x_out = mlp_block(x_loc, [o_full], w_full, w_out, norm_mlp, w_gate, w_up, w_down, tp)
         return x_out, k_new, v_new
 
     row_spec = P(('dp', 'cp'), None)

time: 626 us -> 520 us (0.83)
  Pallas kernels: 535 us -> 470 us
  local copies, waits for them, and re-layouts: 31.1 us -> 14.1 us
  between operations: 14.7 us -> 0.82 us
    pallas_call x2 -> x1, Pallas kernels: 285 us -> 209 us  [attention(): pl.pallas_call(functools.partial(attn_kernel, cfg), grid=(1,), in_specs=[...]
    unnamed x30 -> x25, local copies, waits for them, and re-layouts: 24 us -> 12.2 us
    pallas_call x1, Pallas kernels: 250 us -> 261 us  [mlp_block(): pl.pallas_call(functools.partial(mlp_kernel, dict(tp=tp, n_o=len(o_parts)...]
  transfers between devices with their start and end apart: 1 -> 0, of which waited for: 0 -> 0; matrix products, arithmetic and copies ran while one was open for 9% -> 0% of each run, Pallas kernels for 46% -> 0%
where the time goes in v3:
time: 520 us; the launch traced here: 519 us
  Pallas kernels  470 us (90%)
  matrix products  23.2 us (4%)
  local copies, waits for them, and re-layouts  14.1 us (3%)
  other arithmetic  10.8 us (2%)
    pallas_call x1, Pallas kernels, mlp_block(): pl.pallas_call(functools.partial(mlp_kernel, dict(tp=tp, n_o=len(o_parts)...  261 us
    pallas_call x1, Pallas kernels, attention(): pl.pallas_call(functools.partial(attn_kernel, cfg), grid=(1,), in_specs=[...  209 us
    dot_general x1, matrix products, local_layer(): q_proj = jnp.dot(hidden, w_query, preferred_element_type=jnp.float32)  12.6 us
    unnamed x25, local copies, waits for them, and re-layouts  12.2 us

profile of v3, /device:TPU:96, one launch (start us, length us, event | category | flops | bytes accessed | tf_op | source)
XLA Modules:
  0.0 519.1 jit_solution(12921072350062029908)
XLA Ops:
  0.6 0.0 copy-start.6
  0.6 0.0 copy-start.5
  0.7 0.0 copy-start
  0.7 5.2 %fusion = f32[1024]{0:T(1024)S(1)} fusion(bf16[1024,4096]{1,0:T(8,128)(2,1)} %refs_0_.1), kind=kLoop, calls=%fused_computation.2 | loop fusion | flops 12581888 | bytes 8392704 | tf_op jit(solution)/shard_map/reduce_sum | solution.py:33
  5.9 0.0 copy-done.5
  6.0 0.0 copy-done.6
  6.0 0.6 reshape.107.refs_4_
  6.6 0.0 copy-done
  6.6 4.4 convolution_convert_fusion
  10.9 0.1 copy.29
  11.1 0.1 copy.24
  11.2 1.3 copy.26
  12.4 0.9 copy.31
  13.3 1.1 copy.21
  14.4 6.3 %fusion.10 = f32[1024,256]{0,1:T(8,128)S(1)} fusion(bf16[4096,256]{1,0:T(8,128)(2,1)} %param.17, bf16[1024,4096]{1,0:T(8,128)(2,1)} %refs_0_.1, f32[4096]{0:T(1024)S(1)} %convert_element_type.21, f32[1024]{0:T(1024)S(1)} %add_rsqrt_fusion), kind=kOutput, calls=%fused_computation.27 | convolution fusion | flops 2164260864 | bytes 11554816 | tf_op jit(solution)/shard_map/dot_general | solution.py:588
  20.7 0.1 fusion.14
  20.8 0.3 copy.28
  21.1 0.3 copy.27
  21.5 0.0 copy-start.1
  21.5 0.0 copy-start.2
  21.5 0.0 slice-start
  21.5 1.9 fusion.3
  23.4 0.3 subtract_convert_fusion
  23.7 1.3 pad_maximum_fusion.2
  25.0 0.3 fusion.18
  25.3 0.3 pad_maximum_fusion.4
  25.6 1.3 copy.25
  26.9 1.5 pad_maximum_fusion
  28.4 12.6 %fusion.12.refs_0_ = f32[1024,1024]{1,0:T(8,128)} fusion(bf16[4096,1024]{1,0:T(8,128)(2,1)} %param.16, bf16[1024,4096]{1,0:T(8,128)(2,1)S(1)} %bitcast.23, f32[4096]{0:T(1024)S(1)} %convert_element_type.21, f32[1024]{0:T(1024)S(1)} %add_rsqrt_fusion), kind=kOutput, calls=%fused_computation.28 | convolution fusion | flops 8606711808 | bytes 20992000 | tf_op jit(solution)/shard_map/dot_general | solution.py:591
  41.0 209.4 %attn.1 = (bf16[1024,4096]{1,0:T(8,128)(2,1)}, bf16[4096,4096]{1,0:T(8,128)(2,1)}) custom-call(f32[1024,1024]{1,0:T(8,128)} %fusion.12.refs_0_, f32[1024,128]{1,0:T(8,128)} %get-tuple-element.20.refs_1_, f32[1024,128]{1,0:T(8,128)} %get-tuple-element.21.refs_2_, bf16[2,2048,128]{2,1,0:T(8,128)(2,1)} %get-tuple-element.22.refs_3_, ...), custom_call_target="tpu_custom_call" | custom-call | flops 51539607552 | bytes 16777216 | tf_op jit(solution)/shard_map/attn/pallas_call | solution.py:298
  250.5 260.7 %mlp.1 = bf16[1024,4096]{1,0:T(8,128)(2,1)} custom-call(bf16[1024,4096]{1,0:T(8,128)(2,1)} %refs_0_.1, bf16[1024,4096]{1,0:T(8,128)(2,1)} %get-tuple-element.5.refs_1_, bf16[4096,4096]{1,0:T(8,128)(2,1)} %get-tuple-element.6.refs_2_, bf16[1024,4096]{1,0:T(8,128)(2,1)} %refs_3_.1, bf16[1,4096]{1,0:T(2,128)(2,1)} %reshape.107.refs_4_, ...), custom_call_target="tpu_custom_call" | custom-call | flops 124554051584 | bytes 524288000 | tf_op jit(solution)/shard_map/mlp/pallas_call | solution.py:553
  511.2 7.9 %copy.33 = bf16[1024,4096]{1,0:T(8,128)(2,1)} copy(bf16[1024,4096]{1,0:T(8,128)(2,1)} %mlp.1) | data formatting | bytes 16777216
  (14 shorter events, 0.1 us)
Async XLA Ops:
  0.6 5.3 %copy-start.6 = (bf16[4096]{0:T(1024)(128)(2,1)S(1)}, bf16[4096]{0:T(1024)(128)(2,1)}, u32[]{:S(2)}) copy-start(bf16[4096]{0:T(1024)(128)(2,1)} %param.20) | copy-start | bytes 24580
  0.6 5.3 %copy-start.5 = (bf16[4096]{0:T(1024)(128)(2,1)S(1)}, bf16[4096]{0:T(1024)(128)(2,1)}, u32[]{:S(2)}) copy-start(bf16[4096]{0:T(1024)(128)(2,1)} %param.15) | copy-start | bytes 24580
  0.7 5.9 %copy-start = (bf16[1024,4096]{1,0:T(8,128)(2,1)S(1)}, bf16[1024,4096]{1,0:T(8,128)(2,1)}, u32[]{:S(2)}) copy-start(bf16[1024,4096]{1,0:T(8,128)(2,1)} %refs_0_.1) | copy-start | bytes 25165828
  6.6 5.9 %copy-start.3 = (bf16[1024,2,128]{2,1,0:T(2,128)(2,1)S(1)}, bf16[1024,2,128]{2,1,0:T(2,128)(2,1)}, u32[]{:S(2)}) copy-start(bf16[1024,2,128]{2,1,0:T(2,128)(2,1)} %param.13) | copy-start | bytes 1572868
  6.6 6.7 %copy-start.4 = (bf16[1024,2,128]{2,1,0:T(2,128)(2,1)S(1)}, bf16[1024,2,128]{2,1,0:T(2,128)(2,1)}, u32[]{:S(2)}) copy-start(bf16[1024,2,128]{2,1,0:T(2,128)(2,1)} %param.14) | copy-start | bytes 1572868
  21.5 5.5 %copy-start.1 = (bf16[1024,2,128]{2,0,1:T(8,128)(2,1)S(1)}, bf16[1024,2,128]{2,0,1:T(8,128)(2,1)}, u32[]{:S(2)}) copy-start(bf16[1024,2,128]{2,0,1:T(8,128)(2,1)} %copy.31) | copy-start | bytes 1572868
  21.5 5.4 %copy-start.2 = (bf16[8,128,2,128]{1,3,0,2:T(8,128)(2,1)S(1)}, bf16[8,128,2,128]{1,3,0,2:T(8,128)(2,1)}, u32[]{:S(2)}) copy-start(bf16[8,128,2,128]{1,3,0,2:T(8,128)(2,1)} %copy.21) | copy-start | bytes 1572868
  21.5 7.0 %slice-start = ((s8[8388608]{0:T(1024)(128)(4,1)}), s8[4194304]{0:T(1024)(128)(4,1)S(1)}, s32[]{:S(2)}) async-start(s8[8388608]{0:T(1024)(128)(4,1)} %bitcast.22), calls=%async_computation | async-start | bytes 8388608
  25.0 3.5 slice-start.1

commit v4 on v3

--- a/solution.py
+++ b/solution.py
@@ -10,7 +10,7 @@
 ROPE_THETA = 500000.0
 NORM_EPS = 1e-5
 LOG2E = 1.4426950408889634
-KEY_BLOCK = 512
+UNROLL = 8
 
 
 def rope_tables(positions, head_dim):
@@ -47,10 +47,10 @@
     sib = {'cp': my_x * 2 + (1 - my_core)}
     x_next = {'cp': (me + 2) % groups}
     x_prev = {'cp': (me + groups - 2) % groups}
-    peers = [{'tp': (my_tp + k) % tp} for k in range(1, tp)]
+    above, below = {'tp': (my_tp + 1) % tp}, {'tp': (my_tp + tp - 1) % tp}
 
     barrier = pltpu.get_barrier_semaphore()
-    greet = peers + [sib, x_next, x_prev]
+    greet = [above, below, sib, x_next, x_prev]
     for dev in greet:
         pl.semaphore_signal(barrier, inc=1, device_id=dev, device_id_type=MESH)
     pl.semaphore_wait(barrier, len(greet))
@@ -91,7 +91,6 @@
     w_half = quarter // 2
     my_quarter = 2 * (my_x % 2) + my_core
     x_quarter = 2 * (1 - my_x % 2) + my_core
-    above, below = {'tp': (my_tp + 1) % tp}, {'tp': (my_tp + tp - 1) % tp}
     ks = (tp - 1, 1, 2)
 
     def w_rows(k, which, lo, n):
@@ -166,7 +165,8 @@
 
         last = n_pre + blk if suffix else hi - 1
         if load:
-            state = (st_scr[h, head_dim + 8:head_dim + 9], st_scr[h, head_dim:head_dim + 8], st_scr[h, :head_dim])
+            i = upper * heads + h
+            state = (st_scr[i, head_dim + 8:head_dim + 9], st_scr[i, head_dim:head_dim + 8], st_scr[i, :head_dim])
         else:
             state = (jnp.full((1, rows), -jnp.inf, jnp.float32), jnp.zeros((8, rows), jnp.float32), jnp.zeros((head_dim, rows), jnp.float32))
         s_scr[0] = scores(lo)
@@ -180,44 +180,65 @@
                 return st
             return body
 
-        state = lax.fori_loop(0, (hi - lo) // 4, make_body(lo, 4), state)
+        unroll = UNROLL if (hi - lo) % UNROLL == 0 else 4
+        state = lax.fori_loop(0, (hi - lo) // unroll, make_body(lo, unroll), state)
         if suffix:
-            state = lax.fori_loop(0, blk // 2, make_body(n_pre, 2), state)
-
-            def odd_body(i, st):
-                s_scr[1] = scores(last)
-                return update(s_scr[0], values_t(last - 1), st)
-
-            state = lax.fori_loop(0, blk % 2, odd_body, state)
+            state = lax.fori_loop(0, blk // 4, make_body(n_pre, 4), state)
+
+            def rest_body(i, st):
+                j = last - blk % 4 + i
+                s_scr[(i + 1) % 2] = scores(j + 1)
+                return update(s_scr[i % 2], values_t(j), st)
+
+            state = lax.fori_loop(0, blk % 4, rest_body, state)
             s = s_scr[blk % 2]
             kid = lax.broadcasted_iota(jnp.int32, s.shape, 0)
             qid = lax.broadcasted_iota(jnp.int32, s.shape, 1)
             state = update(jnp.where(kid <= qid, s, -jnp.inf), values_t(last), state)
         m, l, acc = state
         if store:
-            st_scr[h, :head_dim] = acc
-            st_scr[h, head_dim:head_dim + 8] = l
-            st_scr[h, head_dim + 8:] = jnp.broadcast_to(m, (8, rows))
+            i = upper * heads + h
+            st_scr[i, :head_dim] = acc
+            st_scr[i, head_dim:head_dim + 8] = l
+            st_scr[i, head_dim + 8:] = jnp.broadcast_to(m, (8, rows))
         else:
             o_scr[upper * heads + h] = (acc / jnp.sum(l, axis=0, keepdims=True)).T.astype(o_scr.dtype)
 
-    def o_dst(upper, h):
-        return o_full.at[upper * rows:(upper + 1) * rows, pl.ds(pl.multiple_of(my_tp * heads * head_dim + h * head_dim, head_dim), head_dim)]
-
-    def o_copies(upper, h):
+    def o_piece(upper, h, k, lo, n):
+        col = ((my_tp + k) % tp) * heads * head_dim + h * head_dim
+        return o_full.at[upper * rows + lo:upper * rows + lo + n, pl.ds(pl.multiple_of(col, head_dim), head_dim)]
+
+    def o_near(upper, h):
         i = upper * heads + h
-        return [remote(o_scr.at[i], o_dst(upper, h), o_send.at[k, i], o_recv.at[k, i], dev) for k, dev in enumerate(peers)]
+        return [remote(o_scr.at[i], o_piece(upper, h, 0, 0, rows), o_send.at[k, i], o_recv.at[k, i], dev) for k, dev in enumerate((above, below))]
+
+    def o_far(upper, h):
+        i = upper * heads + h
+        n = rows // 2
+        lower_piece, upper_piece = o_piece(upper, h, tp - 1, 0, n), o_piece(upper, h, 1, n, n)
+        return [remote(lower_piece, lower_piece, o_send.at[2, i], o_recv.at[2, i], above), remote(upper_piece, upper_piece, o_send.at[3, i], o_recv.at[3, i], below)]
 
     def o_own(upper, h):
-        return pltpu.make_async_copy(o_scr.at[upper * heads + h], o_dst(upper, h), o_local.at[upper * heads + h])
+        i = upper * heads + h
+        return pltpu.make_async_copy(o_scr.at[i], o_piece(upper, h, 0, 0, rows), o_local.at[i])
+
+    def forward(upper, h):
+        for copy in o_near(upper, h):
+            copy.wait_recv()
+        for copy in o_far(upper, h):
+            copy.start()
 
     def loop_heads(upper, lo_h, hi_h, lo, hi, suffix, load):
         def body(h, carry):
             head_pass(upper, h, lo, hi, suffix, load, not suffix)
             if suffix:
                 o_own(upper, h).start()
-                for copy in o_copies(upper, h):
+                for copy in o_near(upper, h):
                     copy.start()
+
+                @pl.when(h > 0)
+                def _():
+                    forward(upper, h - 1)
             return carry
         lax.fori_loop(lo_h, hi_h, body, 0)
 
@@ -241,26 +262,29 @@
         copy.wait_recv()
     for copy in w_far():
         copy.start()
-    arrived(0, (7,))
-    arrived(1, (4, 5, 6))
-    start(1, (7,))
     for n in range(2):
         w_sib(n, False).start()
         for copy in w_x(n):
             copy.start()
+    loop_heads(1, 0, heads, 0, 8, False, False)
+    arrived(0, (7,))
+    arrived(1, (4, 5, 6))
+    start(1, (7,))
     arrived(1, (7,))
     loop_heads(0, 0, heads, 12, 16, True, True)
+    forward(0, heads - 1)
     for copy in w_far():
         copy.wait_recv()
     w_sib(2, False).start()
     for copy in w_x(2):
         copy.start()
-    loop_heads(1, 0, heads // 2, 0, 16, True, False)
+    loop_heads(1, 0, heads // 2, 8, 16, True, True)
     for n in range(3):
         for copy in w_x(n):
             copy.wait_recv()
         w_sib(n, True).start()
-    loop_heads(1, heads // 2, heads, 0, 16, True, False)
+    loop_heads(1, heads // 2, heads, 8, 16, True, True)
+    forward(1, heads - 1)
 
     for g in gs:
         for part in range(2):
@@ -277,7 +301,9 @@
     for upper in range(2):
         def drain(h, carry):
             o_own(upper, h).wait()
-            for copy in o_copies(upper, h):
+            for copy in o_near(upper, h):
+                copy.wait_send()
+            for copy in o_far(upper, h):
                 copy.wait()
             return carry
         lax.fori_loop(0, heads, drain, 0)
@@ -290,9 +316,9 @@
     any_spec = pl.BlockSpec(memory_space=pl.ANY)
     whole = lambda arr: pl.BlockSpec(arr.shape, lambda i: (0, 0))
     kv_shape = (kv_heads, 2 * groups, 2 * key_rows, head_dim)
-    kv_sem, o_sem = dma((kv_heads, 2 * groups)), dma((tp - 1, 2 * heads))
+    kv_sem, o_sem = dma((kv_heads, 2 * groups)), dma((4, 2 * heads))
     scratch = [pltpu.VMEM(q.shape, bf), pltpu.VMEM(kv_shape, bf), pltpu.VMEM((2, key_rows // 2, rows), f32), pltpu.VMEM((2 * heads, rows, head_dim), bf),
-               pltpu.VMEM((heads, head_dim + 16, rows), f32), kv_sem, kv_sem, o_sem, o_sem, dma((2 * heads,)),
+               pltpu.VMEM((2 * heads, head_dim + 16, rows), f32), kv_sem, kv_sem, o_sem, o_sem, dma((2 * heads,)),
                dma((2,)), dma((2,)), dma((2,)), dma((2,)), dma((2, 3)), dma((2, 3)), dma((2, 3)), dma((2, 3))]
     n_keys = (4 * groups + 2 * groups) * (key_rows // 2)
     return pl.pallas_call(

time: 520 us -> 518 us (level)
    pallas_call x1, Pallas kernels: 261 us -> 252 us  [mlp_block(): pl.pallas_call(functools.partial(mlp_kernel, dict(tp=tp, n_o=len(o_parts)...]
where the time goes in v4:
time: 518 us; the launch traced here: 514 us
  Pallas kernels  465 us (90%)
  matrix products  23.2 us (4%)
  local copies, waits for them, and re-layouts  14.1 us (3%)
  other arithmetic  10.8 us (2%)
    pallas_call x1, Pallas kernels, mlp_block(): pl.pallas_call(functools.partial(mlp_kernel, dict(tp=tp, n_o=len(o_parts)...  252 us
    pallas_call x1, Pallas kernels, attention(): pl.pallas_call(functools.partial(attn_kernel, cfg), grid=(1,), in_specs=[...  213 us
    dot_general x1, matrix products, local_layer(): q_proj = jnp.dot(hidden, w_query, preferred_element_type=jnp.float32)  12.6 us
    unnamed x25, local copies, waits for them, and re-layouts  12.2 us

profile of v4, /device:TPU:96, one launch (start us, length us, event | category | flops | bytes accessed | tf_op | source)
XLA Modules:
  0.0 514.2 jit_solution(15184466158862573589)
XLA Ops:
  0.6 0.0 copy-start.6
  0.6 0.0 copy-start.5
  0.7 0.0 copy-start
  0.7 5.2 %fusion = f32[1024]{0:T(1024)S(1)} fusion(bf16[1024,4096]{1,0:T(8,128)(2,1)} %refs_0_.1), kind=kLoop, calls=%fused_computation.2 | loop fusion | flops 12581888 | bytes 8392704 | tf_op jit(solution)/shard_map/reduce_sum | solution.py:33
  5.9 0.0 copy-done.5
  6.0 0.0 copy-done.6
  6.0 0.6 reshape.107.refs_4_
  6.6 0.0 copy-done
  6.6 4.4 convolution_convert_fusion
  10.9 0.1 copy.29
  11.1 0.1 copy.24
  11.2 1.3 copy.26
  12.4 0.9 copy.31
  13.3 1.1 copy.21
  14.4 6.3 %fusion.10 = f32[1024,256]{0,1:T(8,128)S(1)} fusion(bf16[4096,256]{1,0:T(8,128)(2,1)} %param.17, bf16[1024,4096]{1,0:T(8,128)(2,1)} %refs_0_.1, f32[4096]{0:T(1024)S(1)} %convert_element_type.21, f32[1024]{0:T(1024)S(1)} %add_rsqrt_fusion), kind=kOutput, calls=%fused_computation.27 | convolution fusion | flops 2164260864 | bytes 11554816 | tf_op jit(solution)/shard_map/dot_general | solution.py:614
  20.7 0.1 fusion.14
  20.8 0.3 copy.28
  21.1 0.3 copy.27
  21.5 0.0 copy-start.2
  21.5 0.0 slice-start
  21.5 1.9 fusion.3
  23.4 0.3 subtract_convert_fusion
  23.7 1.3 pad_maximum_fusion.2
  25.0 0.3 fusion.18
  25.3 0.3 pad_maximum_fusion.4
  25.6 1.3 copy.25
  26.9 0.0 copy-done.1
  26.9 1.5 pad_maximum_fusion
  28.4 12.6 %fusion.12.refs_0_ = f32[1024,1024]{1,0:T(8,128)} fusion(bf16[4096,1024]{1,0:T(8,128)(2,1)} %param.16, bf16[1024,4096]{1,0:T(8,128)(2,1)S(1)} %bitcast.23, f32[4096]{0:T(1024)S(1)} %convert_element_type.21, f32[1024]{0:T(1024)S(1)} %add_rsqrt_fusion), kind=kOutput, calls=%fused_computation.28 | convolution fusion | flops 8606711808 | bytes 20992000 | tf_op jit(solution)/shard_map/dot_general | solution.py:617
  41.0 213.0 %attn.1 = (bf16[1024,4096]{1,0:T(8,128)(2,1)}, bf16[4096,4096]{1,0:T(8,128)(2,1)}) custom-call(f32[1024,1024]{1,0:T(8,128)} %fusion.12.refs_0_, f32[1024,128]{1,0:T(8,128)} %get-tuple-element.20.refs_1_, f32[1024,128]{1,0:T(8,128)} %get-tuple-element.21.refs_2_, bf16[2,2048,128]{2,1,0:T(8,128)(2,1)} %get-tuple-element.22.refs_3_, ...), custom_call_target="tpu_custom_call" | custom-call | flops 51539607552 | bytes 16777216 | tf_op jit(solution)/shard_map/attn/pallas_call | solution.py:324
  254.1 251.7 %mlp.1 = bf16[1024,4096]{1,0:T(8,128)(2,1)} custom-call(bf16[1024,4096]{1,0:T(8,128)(2,1)} %refs_0_.1, bf16[1024,4096]{1,0:T(8,128)(2,1)} %get-tuple-element.5.refs_1_, bf16[4096,4096]{1,0:T(8,128)(2,1)} %get-tuple-element.6.refs_2_, bf16[1024,4096]{1,0:T(8,128)(2,1)} %refs_3_.1, bf16[1,4096]{1,0:T(2,128)(2,1)} %reshape.107.refs_4_, ...), custom_call_target="tpu_custom_call" | custom-call | flops 124554051584 | bytes 524288000 | tf_op jit(solution)/shard_map/mlp/pallas_call | solution.py:579
  505.8 7.9 %copy.33 = bf16[1024,4096]{1,0:T(8,128)(2,1)} copy(bf16[1024,4096]{1,0:T(8,128)(2,1)} %mlp.1) | data formatting | bytes 16777216
  (14 shorter events, 0.1 us)
Async XLA Ops:
  0.6 5.3 %copy-start.6 = (bf16[4096]{0:T(1024)(128)(2,1)S(1)}, bf16[4096]{0:T(1024)(128)(2,1)}, u32[]{:S(2)}) copy-start(bf16[4096]{0:T(1024)(128)(2,1)} %param.20) | copy-start | bytes 24580
  0.6 5.3 %copy-start.5 = (bf16[4096]{0:T(1024)(128)(2,1)S(1)}, bf16[4096]{0:T(1024)(128)(2,1)}, u32[]{:S(2)}) copy-start(bf16[4096]{0:T(1024)(128)(2,1)} %param.15) | copy-start | bytes 24580
  0.7 5.9 %copy-start = (bf16[1024,4096]{1,0:T(8,128)(2,1)S(1)}, bf16[1024,4096]{1,0:T(8,128)(2,1)}, u32[]{:S(2)}) copy-start(bf16[1024,4096]{1,0:T(8,128)(2,1)} %refs_0_.1) | copy-start | bytes 25165828
  6.6 5.9 %copy-start.3 = (bf16[1024,2,128]{2,1,0:T(2,128)(2,1)S(1)}, bf16[1024,2,128]{2,1,0:T(2,128)(2,1)}, u32[]{:S(2)}) copy-start(bf16[1024,2,128]{2,1,0:T(2,128)(2,1)} %param.13) | copy-start | bytes 1572868
  6.6 6.7 %copy-start.4 = (bf16[1024,2,128]{2,1,0:T(2,128)(2,1)S(1)}, bf16[1024,2,128]{2,1,0:T(2,128)(2,1)}, u32[]{:S(2)}) copy-start(bf16[1024,2,128]{2,1,0:T(2,128)(2,1)} %param.14) | copy-start | bytes 1572868
  21.5 5.5 %copy-start.1 = (bf16[1024,2,128]{2,0,1:T(8,128)(2,1)S(1)}, bf16[1024,2,128]{2,0,1:T(8,128)(2,1)}, u32[]{:S(2)}) copy-start(bf16[1024,2,128]{2,0,1:T(8,128)(2,1)} %copy.31) | copy-start | bytes 1572868
  21.5 5.4 %copy-start.2 = (bf16[8,128,2,128]{1,3,0,2:T(8,128)(2,1)S(1)}, bf16[8,128,2,128]{1,3,0,2:T(8,128)(2,1)}, u32[]{:S(2)}) copy-start(bf16[8,128,2,128]{1,3,0,2:T(8,128)(2,1)} %copy.21) | copy-start | bytes 1572868
  21.5 7.0 %slice-start = ((s8[8388608]{0:T(1024)(128)(4,1)}), s8[4194304]{0:T(1024)(128)(4,1)S(1)}, s32[]{:S(2)}) async-start(s8[8388608]{0:T(1024)(128)(4,1)} %bitcast.22), calls=%async_computation | async-start | bytes 8388608
  25.0 3.5 slice-start.1
